TPU v7x, 256 devices: a whole 4x4x8 slice. The times are simulated.
256 devices in a mesh: group: 4 (over x), shard: 64 (over y, z, core).
Axes of the slice: x: 4, y: 4, z: 8, core: 2. Of those that a mesh axis runs over, the one named last changes fastest.
Arguments:
- table: bfloat16 [2, 524288, 128], P(None, 'shard'), may hold values from -3 to 3
- owners: int32 [4, 2, 2, 32768, 1], P('group', None, None, 'shard'), may hold values from 0 to 63; in each aligned block of 512 rows (0 to 511, 512 to 1023, ..., all dimensions but the last counted through in order) at most 24 rows name the same one
- offsets: int32 [4, 2, 2, 32768], P('group', None, None, 'shard'), may hold values from 0 to 8191
- bag_lengths: int32 [4, 2, 2, 64, 128], P('group', None, None, 'shard'), may hold values from 1 to 16, 512 in all within a row
- dense_feats: float32 [4, 2, 8192, 13], P('group', None, 'shard'), may hold values from -6 to 6
- labels: int32 [4, 2, 8192], P('group', None, 'shard'), may hold values 0 or 1
- bottom_weight: float32 [13, 128], replicated, may hold values from -1.75 to 1.75
- top_weight: float32 [384, 1024], P('shard'), may hold values from -0.3125 to 0.3125
- out_weight: float32 [1024], replicated, may hold values from -1 to 1
- client_group: int32 [16], replicated, may hold values from 0 to 3
Outputs:
- emb_delta: float32 [2, 524288, 128], P(None, 'shard')
- top_delta: float32 [384, 1024], P('shard')
- bottom_delta: float32 [13, 128], replicated
- out_delta: float32 [1024], replicated
Inputs may be any that keep to these rules, and one draw needn't show every extreme that they name: `owners`: in each device's block of 512 lookups of one group, step and table, no owner is named by more than 24 lookups. `bag_lengths`: the 128 bag sizes of one device, group, step and table sum to 512.
All inputs are finite; a program needn't handle non-finite values. No bound on the sum of `labels` on one device may be relied on, other than what follows from the above.
Results may differ from a plain program's by a relative error of at most 0.008.
Values may be sent and summed in bfloat16 or wider, within the bound.
No kernel may reach another device: no remote copies, remote signals or barrier semaphores. Data moves between devices by JAX's collectives and lax.ppermute only.
A program may use at most 128 MiB of HBM per device.

v0:
```python
import jax
import jax.numpy as jnp
from jax import lax
from jax.experimental import pallas as pl
from jax.experimental.pallas import tpu as pltpu
from jax.sharding import PartitionSpec as P

emb_rate = 2.0
dense_rate = 0.5
bf16 = jnp.bfloat16
f32 = jnp.float32
i32 = jnp.int32

NS = 64
NG = 4
ZS, YS = 8, 4
CAP = 24
SLOTS = 2 * CAP
LOOKS = 512
SAMPLES = 128
EMB = 128
ROWS = 8192
HID = 1024
DENSE = 13
ALL_SLOTS = NS * SLOTS
BATCH = NS * SAMPLES

z_groups = [[y * 16 + z * 2 + c for z in range(ZS)] for y in range(YS) for c in range(2)]
y_groups = [[y * 16 + z * 2 + c for y in range(YS)] for z in range(ZS) for c in range(2)]


def params(mb=48):
    return pltpu.CompilerParams(vmem_limit_bytes=mb * 1024 * 1024)


vm = pl.BlockSpec(memory_space=pltpu.VMEM)
sm = pl.BlockSpec(memory_space=pltpu.SMEM)
hb = pl.BlockSpec(memory_space=pl.ANY)


def iota(shape, dim):
    return lax.broadcasted_iota(i32, shape, dim)


def ones_where(mask):
    return jnp.where(mask, 1.0, 0.0).astype(bf16)


def mm(a, b):
    return lax.dot_general(a, b, (((1,), (0,)), ((), ())), preferred_element_type=f32)


def mm_nt(a, b):
    return lax.dot_general(a, b, (((1,), (1,)), ((), ())), preferred_element_type=f32)


def mm_tn(a, b):
    return lax.dot_general(a, b, (((0,), (0,)), ((), ())), preferred_element_type=f32)


def route_kernel(me_ref, own_ref, off_ref, req_ref, slot_ref):
    earlier = ones_where(iota((LOOKS, LOOKS), 0) < iota((LOOKS, LOOKS), 1))
    total = jnp.zeros((NS, 2 * SLOTS), f32)
    count = jnp.zeros((NS, 2 * SLOTS), f32)
    for st in range(4):
        own = own_ref[st : st + 1, :]
        off = off_ref[st : st + 1, :]
        named = iota((NS, LOOKS), 0) == own
        before = mm(ones_where(named), earlier)
        rank = jnp.sum(jnp.where(named, before, 0.0), axis=0, keepdims=True).astype(i32)
        column = ones_where(iota((2 * SLOTS, LOOKS), 0) == rank + st * CAP)
        high = jnp.where(named, (off >> 8).astype(f32), 0.0).astype(bf16)
        low = jnp.where(named, (off & 255).astype(f32), 0.0).astype(bf16)
        total = total + mm_nt(high, column) * 256.0 + mm_nt(low, column)
        count = count + mm_nt(ones_where(named), column)
        slot_ref[st : st + 1, :] = own * SLOTS + (st % 2) * CAP + rank
    spare = me_ref[0] * CAP + iota((NS, 2 * SLOTS), 1) % CAP
    req_ref[...] = jnp.where(count > 0.5, total.astype(i32), spare)


def route(me, own, off):
    return pl.pallas_call(
        route_kernel,
        name="route",
        in_specs=[sm, vm, vm],
        out_specs=[vm, vm],
        out_shape=[
            jax.ShapeDtypeStruct((NS, 2 * SLOTS), i32),
            jax.ShapeDtypeStruct((4, LOOKS), i32),
        ],
        compiler_params=params(),
    )(me, own, off)


def pool_kernel(slot_ref, bag_ref, a_ref, at_ref):
    upto = ones_where(iota((SAMPLES, SAMPLES), 1) <= iota((SAMPLES, SAMPLES), 0))
    below = ones_where(iota((SAMPLES, SAMPLES), 1) < iota((SAMPLES, SAMPLES), 0))
    look = iota((SAMPLES, LOOKS), 1).astype(f32)
    for t in range(2):
        lens = jnp.broadcast_to(bag_ref[t : t + 1, :], (8, SAMPLES)).astype(f32).astype(bf16)
        ends = mm_nt(upto, lens)[:, :1]
        starts = mm_nt(below, lens)[:, :1]
        member = ones_where((look >= starts) & (look < ends))
        slot = slot_ref[t : t + 1, :]
        for q in range(ALL_SLOTS // LOOKS):
            at_slot = ones_where(iota((LOOKS, LOOKS), 0) + q * LOOKS == slot)
            a_ref[t * SAMPLES : (t + 1) * SAMPLES, q * LOOKS : (q + 1) * LOOKS] = mm_nt(
                member, at_slot
            ).astype(bf16)
            at_ref[q * LOOKS : (q + 1) * LOOKS, t * SAMPLES : (t + 1) * SAMPLES] = mm_nt(
                at_slot, member
            ).astype(bf16)


def pool_matrix(slot, bags):
    return pl.pallas_call(
        pool_kernel,
        name="pool_matrix",
        in_specs=[vm, vm],
        out_specs=[vm, vm],
        out_shape=[
            jax.ShapeDtypeStruct((2 * SAMPLES, ALL_SLOTS), bf16),
            jax.ShapeDtypeStruct((ALL_SLOTS, 2 * SAMPLES), bf16),
        ],
        compiler_params=params(),
    )(slot, bags)


def clash_kernel(idx_ref, out_ref):
    idx = idx_ref[...]
    lane = iota(idx.shape, 1)
    clash = jnp.zeros(idx.shape, i32)
    for d in range(1, 8):
        same = (idx == jnp.concatenate([idx[:, -d:], idx[:, :-d]], axis=1)) & (lane % 8 >= d)
        clash = clash | jnp.where(same, 1, 0)
    first = jnp.max(jnp.where(lane < SLOTS, clash, 0), axis=1, keepdims=True)
    second = jnp.max(jnp.where(lane >= SLOTS, clash, 0), axis=1, keepdims=True)
    out_ref[...] = jnp.where(iota((idx.shape[0], 2), 1) == 0, first, second)


def clashes(idx):
    return pl.pallas_call(
        clash_kernel,
        name="clashes",
        in_specs=[vm],
        out_specs=vm,
        out_shape=jax.ShapeDtypeStruct((idx.shape[0], 2), i32),
        compiler_params=params(),
    )(idx)


def gather_rows(idx_ref, first, tables, stage, out_ref):
    def one(s, _):
        base = pl.multiple_of(s * SLOTS, 8)
        for j in range(SLOTS):
            row = idx_ref[s, first + j]
            stage[pl.ds(base + j, 1), :] = tables[j // CAP][pl.ds(row, 1), :]
        return 0

    lax.fori_loop(0, NS, one, 0)
    out_ref[...] = stage[...].astype(bf16)


def add_rows(idx_ref, base_idx, first, clash_ref, step, stage, tables):
    def one(s, _):
        base = pl.multiple_of(s * SLOTS, 8)
        source = base_idx + s
        clear = clash_ref[source, step] == 0

        @pl.when(clear)
        def _():
            for b in range(0, CAP, 8):
                held = []
                for t in range(2):
                    for j in range(8):
                        at = t * CAP + b + j
                        row = idx_ref[source, first + at]
                        held.append((t, row, tables[t][pl.ds(row, 1), :] + stage[pl.ds(base + at, 1), :]))
                for t, row, value in held:
                    tables[t][pl.ds(row, 1), :] = value

        @pl.when(jnp.logical_not(clear))
        def _():
            for at in range(SLOTS):
                table = tables[at // CAP]
                row = idx_ref[source, first + at]
                table[pl.ds(row, 1), :] = table[pl.ds(row, 1), :] + stage[pl.ds(base + at, 1), :]

        return 0

    lax.fori_loop(0, NS, one, 0)


def gather_kernel(idx_ref, tab_ref, out_ref, stage):
    gather_rows(idx_ref, 0, [tab_ref.at[0], tab_ref.at[1]], stage, out_ref)


def gather_first(idx, table32):
    return pl.pallas_call(
        gather_kernel,
        name="gather_first",
        in_specs=[sm, vm],
        out_specs=vm,
        out_shape=jax.ShapeDtypeStruct((ALL_SLOTS, EMB), bf16),
        scratch_shapes=[pltpu.VMEM((ALL_SLOTS, EMB), f32)],
        compiler_params=params(),
    )(idx, table32)


def owner_kernel(idx_ref, clash_ref, grad_ref, tab_ref, out_ref, new0, new1, stage, sems):
    copies = [
        pltpu.make_async_copy(tab_ref.at[t], new, sems.at[t]) for t, new in enumerate((new0, new1))
    ]
    for c in copies:
        c.start()
    stage[...] = grad_ref[...].astype(f32) * -emb_rate
    for c in copies:
        c.wait()
    add_rows(idx_ref, 0, 0, clash_ref, 0, stage, [new0, new1])
    gather_rows(idx_ref, SLOTS, [new0, new1], stage, out_ref)


def owner_step(idx, clash, grads, table32):
    return pl.pallas_call(
        owner_kernel,
        name="owner_step",
        in_specs=[sm, sm, vm, hb],
        out_specs=vm,
        out_shape=jax.ShapeDtypeStruct((ALL_SLOTS, EMB), bf16),
        scratch_shapes=[
            pltpu.VMEM((ROWS, EMB), f32),
            pltpu.VMEM((ROWS, EMB), f32),
            pltpu.VMEM((ALL_SLOTS, EMB), f32),
            pltpu.SemaphoreType.DMA((2,)),
        ],
        compiler_params=params(),
    )(idx, clash, grads, table32)


def make_total_kernel(step):
    def total_kernel(me_ref, weight_ref, idx_ref, clash_ref, *refs):
        refs = list(refs)
        lists = [refs.pop(0) for _ in range(NG)]
        old = refs.pop(0) if step else None
        out_ref = refs.pop(0)
        part, stage, sem, old_sem = refs
        group = me_ref[1]
        if step:
            seed = pltpu.make_async_copy(old, out_ref, old_sem)
            seed.start()
            seed.wait()
        else:
            out_ref[...] = jnp.zeros(out_ref.shape, f32)

        def one(k, _):
            apart = (group + NG - k) % NG
            for d in range(NG):

                @pl.when(apart == d)
                def _(d=d):
                    copy = pltpu.make_async_copy(lists[d], part, sem)
                    copy.start()
                    copy.wait()

            stage[...] = part[...].astype(f32) * weight_ref[k]
            add_rows(
                idx_ref, k * NS, step * SLOTS, clash_ref, step, stage, [out_ref.at[0], out_ref.at[1]]
            )
            return 0

        lax.fori_loop(0, NG, one, 0)

    return total_kernel


def add_lists(me, weights, idx, clash, lists, old, step):
    operands = [me, weights, idx, clash, *lists] + ([old] if step else [])
    return pl.pallas_call(
        make_total_kernel(step),
        name="add_lists_%d" % step,
        in_specs=[sm, sm, sm, sm] + [hb] * (len(operands) - 4),
        out_specs=vm,
        out_shape=jax.ShapeDtypeStruct((2, ROWS, EMB), f32),
        scratch_shapes=[
            pltpu.VMEM((ALL_SLOTS, EMB), bf16),
            pltpu.VMEM((ALL_SLOTS, EMB), f32),
            pltpu.SemaphoreType.DMA,
            pltpu.SemaphoreType.DMA,
        ],
        compiler_params=params(),
    )(*operands)


def top_pick(core):
    row = iota((384, 256), 1)
    device = 2 * (row // 8) + core
    inside = row % 8
    return ones_where((inside < 6) & (device * 6 + inside == iota((384, 256), 0)))


def rest_pick(core):
    row = iota((32, 256), 1)
    return ones_where((row % 8 == 6) & (2 * (row // 8) + core == iota((32, 256), 0)))


def sigmoid(v):
    return 1.0 / (1.0 + jnp.exp(-v))


def make_dense_kernel(step):
    def dense_kernel(
        me_ref, rep_ref, a_ref, at_ref, feat_ref, lab_ref, wa_ref, wb_ref, *refs
    ):
        refs = list(refs)
        core = me_ref[2]
        wa = wa_ref[...]
        wb = wb_ref[...]
        w = (mm(top_pick(core), wa) + mm(top_pick(1 - core), wb)).astype(bf16)
        if step:
            rest = mm(rest_pick(core), wa[:, :384]) + mm(rest_pick(1 - core), wb[:, :384])
            rest = rest[:, :128] + rest[:, 128:256] + rest[:, 256:384]
        else:
            rest = refs.pop(0)[...]
        hold_ref, joined_ref, dpre_ref, grad_ref = refs
        out_row = jnp.concatenate([rest[DENSE + k : DENSE + k + 1, :] for k in range(8)], axis=1)
        feats = feat_ref[...]
        bpre = jnp.zeros((SAMPLES, EMB), f32)
        for k in range(DENSE):
            bpre = bpre + feats[:, k : k + 1] * rest[k : k + 1, :]
        bgate = sigmoid(bpre)
        bottom = bpre * bgate
        pooled = mm(a_ref[...], rep_ref[...])
        joined = jnp.concatenate([bottom, pooled[:SAMPLES], pooled[SAMPLES:]], axis=1).astype(bf16)
        pre = mm(joined, w)
        gate = sigmoid(pre)
        hidden = pre * gate
        logit = jnp.sum(hidden * out_row, axis=1, keepdims=True)
        dlogit = sigmoid(logit) - lab_ref[...]
        dpre = (dlogit * out_row * (gate * (1.0 + pre * (1.0 - gate)))).astype(bf16)
        dz = mm_nt(dpre, w)
        both = jnp.concatenate([dz[:, EMB : 2 * EMB], dz[:, 2 * EMB :]], axis=0).astype(bf16)
        hold_ref[...] = mm(at_ref[...], both).astype(bf16)
        joined_ref[...] = joined
        dpre_ref[...] = dpre
        dbottom = dz[:, :EMB] * (bgate * (1.0 + bpre * (1.0 - bgate)))
        for k in range(DENSE):
            grad_ref[k : k + 1, :] = jnp.sum(feats[:, k : k + 1] * dbottom, axis=0, keepdims=True)
        dout = jnp.sum(hidden * dlogit, axis=0, keepdims=True)
        for k in range(8):
            grad_ref[DENSE + k : DENSE + k + 1, :] = dout[:, k * EMB : (k + 1) * EMB]
        grad_ref[DENSE + 8 :, :] = jnp.zeros((32 - DENSE - 8, EMB), f32)

    return dense_kernel


def dense_step(me, rep, a, at, feats, labels, wa, wb, rest, step):
    operands = [me, rep, a, at, feats, labels, wa, wb] + ([] if step else [rest])
    return pl.pallas_call(
        make_dense_kernel(step),
        name="dense_%d" % step,
        in_specs=[sm] + [vm] * (len(operands) - 1),
        out_specs=[vm] * 4,
        out_shape=[
            jax.ShapeDtypeStruct((ALL_SLOTS, EMB), bf16),
            jax.ShapeDtypeStruct((SAMPLES, 384), bf16),
            jax.ShapeDtypeStruct((SAMPLES, HID), bf16),
            jax.ShapeDtypeStruct((32, EMB), f32),
        ],
        compiler_params=params(),
    )(*operands)


def weight_grad_kernel(me_ref, joined_ref, dpre_ref, rest_ref, keep_ref, send_ref):
    core = me_ref[2]
    joined = joined_ref[...]
    dpre = dpre_ref[...]
    rest = rest_ref[...].astype(bf16)
    for which, out in ((core, keep_ref), (1 - core, send_ref)):
        picked = mm(joined, top_pick(which)).astype(bf16)
        out[...] = mm_tn(picked, dpre).astype(out.dtype)
        more = mm_tn(rest_pick(which), rest)
        out[:, :EMB] = (out[:, :EMB].astype(f32) + more).astype(out.dtype)


def weight_grad(me, joined, dpre, rest):
    return pl.pallas_call(
        weight_grad_kernel,
        name="weight_grad",
        in_specs=[sm, vm, vm, vm],
        out_specs=[vm, vm],
        out_shape=[
            jax.ShapeDtypeStruct((256, HID), f32),
            jax.ShapeDtypeStruct((256, HID), bf16),
        ],
        compiler_params=params(),
    )(me, joined, dpre, rest)


def exchange(x, axis="shard", groups=None):
    return lax.all_to_all(x, axis, 0, 0, tiled=True, axis_index_groups=groups)


def other_core(x):
    return lax.ppermute(x, "shard", [(i, i ^ 1) for i in range(NS)])


def to_group(x, d):
    return lax.ppermute(x, "group", [(i, (i + d) % NG) for i in range(NG)])


def from_groups(x):
    return [x] + [to_group(x, d) for d in range(1, NG)]


def spread(block):
    z = exchange(jnp.broadcast_to(block[None], (ZS, 8, HID)), groups=z_groups)
    y = exchange(
        jnp.broadcast_to(z.reshape(1, 64, HID), (YS, 64, HID)), groups=y_groups
    ).reshape(256, HID)
    return y, other_core(y)


def summed(keep, send):
    half = (keep + other_core(send).astype(f32)).astype(bf16).reshape(YS, 64, HID)
    y = exchange(half, groups=y_groups).astype(f32).sum(axis=0)
    z = exchange(y.astype(bf16).reshape(ZS, 8, HID), groups=z_groups)
    return z.astype(f32).sum(axis=0)


def in_three(v):
    a = lax.reduce_precision(v, 8, 7)
    b = lax.reduce_precision(v - a, 8, 7)
    c = v - a - b
    return a, b, c


def body(
    table,
    owners,
    offsets,
    bag_lengths,
    dense_feats,
    labels,
    bottom_weight,
    top_weight,
    out_weight,
    client_group,
):
    shard = lax.axis_index("shard")
    group = lax.axis_index("group")
    me = jnp.stack([shard, group, shard % 2]).astype(i32)
    counts = jnp.sum((client_group[None, :] == jnp.arange(NG)[:, None]).astype(f32), axis=1)
    weights = counts * NG / client_group.shape[0]
    requests, slots = route(me, owners.reshape(4, LOOKS), offsets.reshape(4, LOOKS))
    rest = jnp.concatenate(
        [bottom_weight, out_weight.reshape(8, EMB), jnp.zeros((NS - DENSE - 8, EMB), f32)], 0
    )
    my_rest = lax.dynamic_slice_in_dim(rest, shard, 1, 0)
    received = exchange(requests)
    idx_all = exchange(jnp.broadcast_to(received[None], (NG, NS, 2 * SLOTS)), "group")
    idx_all = idx_all.reshape(NG * NS, 2 * SLOTS)
    wa, wb = spread(jnp.pad(top_weight, ((0, 2), (0, 0))).astype(bf16))
    matrices = [
        pool_matrix(slots[2 * s : 2 * s + 2], bag_lengths[0, s, :, 0]) for s in range(2)
    ]
    table32 = table.astype(f32)
    own_clash = clashes(received)
    clash_all = clashes(idx_all)
    served = gather_first(received, table32)
    total = None
    top_sum = jnp.zeros((8, HID), f32)
    for step in range(2):
        replies = exchange(served.reshape(NS, SLOTS, EMB)).reshape(ALL_SLOTS, EMB)
        hold, joined, dpre, rest_grad = dense_step(
            me,
            replies,
            *matrices[step],
            dense_feats[0, step],
            labels[0, step].astype(f32)[:, None],
            wa,
            wb,
            rest[:32],
            step,
        )
        grads = exchange(hold.reshape(NS, SLOTS, EMB)).reshape(ALL_SLOTS, EMB)
        top_grad = summed(*weight_grad(me, joined, dpre, rest_grad))
        top_sum = top_sum + top_grad
        if step == 0:
            served = owner_step(received, own_clash, grads, table32)
            new = jnp.pad(top_weight, ((0, 2), (0, 0))) - dense_rate * (top_grad / BATCH)
            parts = in_three(my_rest - dense_rate * (top_grad[6:7, :EMB] / BATCH))
            row = jnp.concatenate([*parts, jnp.zeros((1, HID - 3 * EMB), f32)], 1)
            block = jnp.concatenate([new[:6], row, jnp.zeros((1, HID), f32)], 0)
            wa, wb = spread(block.astype(bf16))
        lists = from_groups(grads)
        total = add_lists(me, -emb_rate * weights, idx_all, clash_all, lists, total, step)
    mine = weights[group] * (-dense_rate / BATCH) * top_sum
    a, b, c, d = from_groups(mine)
    dense = (a + c) + (b + d)
    ends = exchange(jnp.broadcast_to(dense[6:7, :EMB][None], (NS, 1, EMB))).reshape(NS, EMB)
    return (
        total,
        dense[:6],
        ends[:DENSE],
        ends[DENSE : DENSE + 8].reshape(HID),
    )


def solution(mesh):
    in_specs = (
        P(None, "shard", None),
        P("group", None, None, "shard", None),
        P("group", None, None, "shard"),
        P("group", None, None, "shard", None),
        P("group", None, "shard", None),
        P("group", None, "shard"),
        P(),
        P("shard", None),
        P(),
        P(),
    )
    out_specs = (P(None, "shard", None), P("shard", None), P(), P())
    return jax.shard_map(body, mesh=mesh, in_specs=in_specs, out_specs=out_specs, check_vma=False)
```

profile of v0, /device:TPU:1, one launch (start us, length us, event | category | flops | bytes accessed | tf_op | source)
XLA Modules:
  0.0 421.7 jit_solution(15568425143220208939)
XLA Ops:
  0.6 0.7 reduce.2
  1.4 0.7 reshape.126.off_ref
  2.2 2.5 route.1
  4.7 13.1 %all-to-all-start = ((s32[64,1,96]{2,1,0:T(1,128)}), s32[64,1,96]{2,1,0:T(1,128)S(1)}, u32[]{:S(2)}, u32[]{:S(2)}) async-start(s32[64,1,96]{2,1,0:T(1,128)} %bitcast.4), calls=%async_computation | async-start | bytes 65536 | tf_op jit(solution)/shard_map/all_to_all | solution.py:400
  17.8 0.8 pad_convert_fusion
  18.6 8.5 %all-to-all-done = s32[64,1,96]{2,1,0:T(1,128)S(1)} async-done(((s32[64,1,96]{2,1,0:T(1,128)}), s32[64,1,96]{2,1,0:T(1,128)S(1)}, u32[]{:S(2)}, u32[]{:S(2)}) %all-to-all-start) | async-done | bytes 24608 | tf_op jit(solution)/shard_map/all_to_all | solution.py:400
  27.1 10.2 %all_to_all.78 = bf16[8,8,1024]{2,1,0:T(8,128)(2,1)S(1)} all-to-all(bf16[8,8,1024]{2,1,0:T(8,128)(2,1)S(1)} %broadcast_in_dim.28), channel_id=1, replica_groups={{0,2,4,6,8,10,12,14},{1,3,5,7,9,11,13,15},{16,18,20,22,24,26,28,30},{17..., dimensions={0} | all-to-all | bytes 262144 | tf_op jit(solution)/shard_map/all_to_all | solution.py:400
  37.3 0.9 broadcast_in_dim.59
  38.2 3.5 all-to-all-start.4
  41.7 6.1 %convert_element_type.66.tab_ref = f32[2,8192,128]{2,1,0:T(8,128)} convert(bf16[2,8192,128]{2,1,0:T(8,128)(2,1)} %param.10) | non-fusion elementwise | flops 2097152 | bytes 12582912 | tf_op jit(solution)/shard_map/convert_element_type | solution.py:466
  47.8 7.2 %gather_first.1 = bf16[3072,128]{1,0:T(8,128)(2,1)} custom-call(s32[64,96]{1,0:T(8,128)S(1)} %bitcast.63, f32[2,8192,128]{2,1,0:T(8,128)} %convert_element_type.66.tab_ref), custom_call_target="tpu_custom_call" | custom-call | tf_op jit(solution)/shard_map/gather_first/pallas_call | solution.py:199
  55.0 7.5 %all-to-all-start.2 = ((bf16[64,48,128]{2,1,0:T(8,128)(2,1)}), bf16[64,48,128]{2,1,0:T(8,128)(2,1)S(1)}, u32[]{:S(2)}, u32[]{:S(2)}) async-start(bf16[64,48,128]{2,1,0:T(8,128)(2,1)} %bitcast.7), calls=%async_computation.2 | async-start | bytes 1572864 | tf_op jit(solution)/shard_map/all_to_all | solution.py:400
  63.4 0.7 copy.30.lab_ref
  64.2 4.0 pool_matrix.2
  68.1 1.2 copy-done
  69.3 16.1 %all-to-all-done.2 = bf16[64,48,128]{2,1,0:T(8,128)(2,1)S(1)} async-done(((bf16[64,48,128]{2,1,0:T(8,128)(2,1)}), bf16[64,48,128]{2,1,0:T(8,128)(2,1)S(1)}, u32[]{:S(2)}, u32[]{:S(2)}) %all-to-all-start.2) | async-done | bytes 786464 | tf_op jit(solution)/shard_map/all_to_all | solution.py:400
  85.4 0.8 copy-done.7
  86.2 3.9 dense_0.1
  90.2 1.4 weight_grad.2
  92.1 1.5 collective-permute-done.1
  93.8 13.0 %all_to_all.79 = bf16[4,64,1024]{2,1,0:T(8,128)(2,1)S(1)} all-to-all(bf16[4,64,1024]{2,1,0:T(8,128)(2,1)S(1)} %bitcast.70), channel_id=1, replica_groups={{0,16,32,48},{1,17,33,49},{2,18,34,50},{3,19,35,51},{4,20,36,52},{5,21,..., dimensions={0} | all-to-all | bytes 1048576 | tf_op jit(solution)/shard_map/all_to_all | solution.py:400
  106.8 0.7 reduce_sum.52
  107.6 3.5 all-to-all-start.8
  111.2 7.7 %all-to-all-done.8 = bf16[8,8,1024]{2,1,0:T(8,128)(2,1)S(1)} async-done(((bf16[8,8,1024]{2,1,0:T(8,128)(2,1)}), bf16[8,8,1024]{2,1,0:T(8,128)(2,1)S(1)}, u32[]{:S(2)}, u32[]{:S(2)}) %all-to-all-start.8) | async-done | bytes 131104 | tf_op jit(solution)/shard_map/all_to_all | solution.py:400
  118.9 0.7 reduce-precision_convert_fusion.1
  119.8 10.4 %all_to_all.80 = bf16[8,8,1024]{2,1,0:T(8,128)(2,1)S(1)} all-to-all(bf16[8,8,1024]{2,1,0:T(8,128)(2,1)S(1)} %broadcast_in_dim.63), channel_id=1, replica_groups={{0,2,4,6,8,10,12,14},{1,3,5,7,9,11,13,15},{16,18,20,22,24,26,28,30},{17..., dimensions={0} | all-to-all | bytes 262144 | tf_op jit(solution)/shard_map/all_to_all | solution.py:400
  130.2 30.5 %all_to_all.81 = bf16[64,48,128]{2,1,0:T(8,128)(2,1)S(1)} all-to-all(bf16[64,48,128]{2,1,0:T(8,128)(2,1)} %bitcast.67), channel_id=1, replica_groups=mesh['group'=4,'shard'=64] {'shard'}, dimensions={0} | all-to-all | bytes 1572864 | tf_op jit(solution)/shard_map/all_to_all | solution.py:400
  160.7 0.9 broadcast_in_dim.65
  161.6 4.1 all-to-all-start.10
  166.0 12.7 %owner_step.1 = bf16[3072,128]{1,0:T(8,128)(2,1)} custom-call(s32[64,96]{1,0:T(8,128)S(1)} %bitcast.65, s32[64,2]{1,0:T(8,128)S(1)} %clashes.3.clash_ref, bf16[3072,128]{1,0:T(8,128)(2,1)S(1)} %bitcast.45, f32[2,8192,128]{2,1,0:T(8,128)} %convert_element_type.66.tab_ref), custom_call_target="tpu_custom_call" | custom-call | tf_op jit(solution)/shard_map/owner_step/pallas_call | solution.py:224
  178.7 7.7 %all-to-all-start.6 = ((bf16[64,48,128]{2,1,0:T(8,128)(2,1)}), bf16[64,48,128]{2,1,0:T(8,128)(2,1)S(1)}, u32[]{:S(2)}, u32[]{:S(2)}) async-start(bf16[64,48,128]{2,1,0:T(8,128)(2,1)} %bitcast.18), calls=%async_computation.6 | async-start | bytes 1572864 | tf_op jit(solution)/shard_map/all_to_all | solution.py:400
  187.1 4.0 pool_matrix.3
  191.1 1.1 copy-done.1
  192.2 1.2 copy-done.3
  193.4 15.9 %all-to-all-done.6 = bf16[64,48,128]{2,1,0:T(8,128)(2,1)S(1)} async-done(((bf16[64,48,128]{2,1,0:T(8,128)(2,1)}), bf16[64,48,128]{2,1,0:T(8,128)(2,1)S(1)}, u32[]{:S(2)}, u32[]{:S(2)}) %all-to-all-start.6) | async-done | bytes 786464 | tf_op jit(solution)/shard_map/all_to_all | solution.py:400
  209.3 1.4 copy-done.2
  210.7 4.9 %dense_1.1 = (bf16[3072,128]{1,0:T(8,128)(2,1)}, bf16[128,384]{1,0:T(8,128)(2,1)S(1)}, bf16[128,1024]{1,0:T(8,128)(2,1)S(1)}, f32[32,128]{1,0:T(8,128)S(1)}) custom-call(s32[3]{0:T(128)S(1)} %pad_add_fusion.me_ref, bf16[3072,128]{1,0:T(8,128)(2,1)S(1)} %bitcast.55, bf16[256,3072]{1,0:T(8,128)(2,1)S(1)} %copy-done.2, bf16[3072,256]{1,0:T(8,128)(2,1)} %copy-done.3, ...), custom_call_target="tpu_custom_call" | custom-call | tf_op jit(solution)/shard_map/dense_1/pallas_call | solution.py:358
  215.6 1.4 weight_grad.3
  217.5 1.5 collective-permute-done.9
  219.2 13.0 %all_to_all.82 = bf16[4,64,1024]{2,1,0:T(8,128)(2,1)S(1)} all-to-all(bf16[4,64,1024]{2,1,0:T(8,128)(2,1)S(1)} %bitcast.71), channel_id=1, replica_groups={{0,16,32,48},{1,17,33,49},{2,18,34,50},{3,19,35,51},{4,20,36,52},{5,21,..., dimensions={0} | all-to-all | bytes 1048576 | tf_op jit(solution)/shard_map/all_to_all | solution.py:400
  232.3 10.4 %all_to_all.83 = bf16[8,8,1024]{2,1,0:T(8,128)(2,1)S(1)} all-to-all(bf16[8,8,1024]{2,1,0:T(8,128)(2,1)S(1)} %bitcast.74), channel_id=1, replica_groups={{0,2,4,6,8,10,12,14},{1,3,5,7,9,11,13,15},{16,18,20,22,24,26,28,30},{17..., dimensions={0} | all-to-all | bytes 262144 | tf_op jit(solution)/shard_map/all_to_all | solution.py:400
  242.8 6.7 %all-to-all-start.11 = ((bf16[64,48,128]{2,1,0:T(8,128)(2,1)}), bf16[64,48,128]{2,1,0:T(8,128)(2,1)S(1)}, u32[]{:S(2)}, u32[]{:S(2)}) async-start(bf16[64,48,128]{2,1,0:T(8,128)(2,1)} %bitcast.27), calls=%async_computation.11 | async-start | bytes 1572864 | tf_op jit(solution)/shard_map/all_to_all | solution.py:400
  249.5 2.8 collective-permute-start.8
  252.4 0.6 dynamic_slice.7
  253.7 0.6 collective-permute-start.12
  254.3 0.9 collective-permute-start.11
  255.7 2.4 collective-permute-start.7
  258.2 10.5 %collective-permute-done.8.refs_3_ = bf16[3072,128]{1,0:T(8,128)(2,1)S(1)} collective-permute-done((bf16[3072,128]{1,0:T(8,128)(2,1)S(1)}, bf16[3072,128]{1,0:T(8,128)(2,1)S(1)}, u32[]{:S(2)}, u32[]{:S(2)}) %collective-permute-start.8) | collective-permute-done | bytes 786464 | tf_op jit(solution)/shard_map/ppermute | solution.py:408
  268.7 0.9 copy-done.4
  269.6 0.8 collective-permute-start.6
  270.4 2.1 all-to-all-done.11
  272.5 17.0 %collective-permute-start.5 = (bf16[3072,128]{1,0:T(8,128)(2,1)S(1)}, bf16[3072,128]{1,0:T(8,128)(2,1)S(1)}, u32[]{:S(2)}, u32[]{:S(2)}) collective-permute-start(bf16[3072,128]{1,0:T(8,128)(2,1)S(1)} %bitcast.50), channel_id=1, source_target_pairs={{0,192},{64,0},{128,64},{192,128},{1,193},{65,1},{129,65},{193,129... | collective-permute-start | bytes 2359304 | tf_op jit(solution)/shard_map/ppermute | solution.py:408
  289.6 0.7 collective-permute-start.3
  290.2 0.7 broadcast_in_dim.27
  290.9 3.6 all-to-all-start.1
  294.5 33.4 %all-to-all-done.1 = s32[4,64,96]{2,1,0:T(8,128)S(1)} async-done(((s32[4,64,96]{2,1,0:T(8,128)}), s32[4,64,96]{2,1,0:T(8,128)S(1)}, u32[]{:S(2)}, u32[]{:S(2)}) %all-to-all-start.1) | async-done | bytes 98336 | tf_op jit(solution)/shard_map/all_to_all | solution.py:400
  327.9 0.6 broadcast_in_dim.67
  328.5 20.4 %all-to-all-start.14 = ((f32[64,1,128]{2,1,0:T(1,128)}), f32[64,1,128]{2,1,0:T(1,128)S(1)}, u32[]{:S(2)}, u32[]{:S(2)}) async-start(f32[64,1,128]{2,1,0:T(1,128)} %broadcast_in_dim.67), calls=%async_computation.14 | async-start | bytes 65536 | tf_op jit(solution)/shard_map/all_to_all | solution.py:400
  348.9 0.9 clashes.2.clash_ref
  349.9 1.1 copy-done.5
  351.0 32.8 %add_lists_0.1.refs_4_ = f32[2,8192,128]{2,1,0:T(8,128)} custom-call(s32[3]{0:T(128)S(1)} %pad_add_fusion.me_ref, f32[4]{0:T(128)S(1)} %get-tuple-element.51.weight_ref, s32[256,96]{1,0:T(8,128)S(1)} %bitcast.57, s32[256,2]{1,0:T(8,128)S(1)} %clashes.2.clash_ref, bf16[3072,128]{1,0:T(8,128)(2,1)S(1)} %bitcast.49, ...), custom_call_target="tpu_custom_call" | custom-call | tf_op jit(solution)/shard_map/add_lists_0/pallas_call | solution.py:278
  383.9 0.6 copy.39
  384.5 0.6 slice.74
  385.1 36.5 %add_lists_1.1 = f32[2,8192,128]{2,1,0:T(8,128)} custom-call(s32[3]{0:T(128)S(1)} %pad_add_fusion.me_ref, f32[4]{0:T(128)S(1)} %get-tuple-element.51.weight_ref, s32[256,96]{1,0:T(8,128)S(1)} %bitcast.58, s32[256,2]{1,0:T(8,128)S(1)} %clashes.2.clash_ref, bf16[3072,128]{1,0:T(8,128)(2,1)S(1)} %bitcast.53, bf16[3072,128]{1,0:T(8,128)(2,1)} %collective-permute-done.3.refs_1_, ...), custom_call_target="tpu_custom_call" | custom-call | tf_op jit(solution)/shard_map/add_lists_1/pallas_call | solution.py:278
  (78 shorter events, 4.5 us)
Async XLA Ops:
  4.7 22.4 %all-to-all-start = ((s32[64,1,96]{2,1,0:T(1,128)}), s32[64,1,96]{2,1,0:T(1,128)S(1)}, u32[]{:S(2)}, u32[]{:S(2)}) async-start(s32[64,1,96]{2,1,0:T(1,128)} %bitcast.4), calls=%async_computation | async-start | bytes 65536 | tf_op jit(solution)/shard_map/all_to_all | solution.py:400
  38.2 16.8 %all-to-all-start.4 = ((bf16[4,64,1024]{2,1,0:T(8,128)(2,1)}), bf16[4,64,1024]{2,1,0:T(8,128)(2,1)S(1)}, u32[]{:S(2)}, u32[]{:S(2)}) async-start(bf16[4,64,1024]{2,1,0:T(8,128)(2,1)} %broadcast_in_dim.59), calls=%async_computation.4 | async-start | bytes 1048576 | tf_op jit(solution)/shard_map/all_to_all | solution.py:400
  47.8 14.8 %copy-start.11 = (f32[1,2,128,13]{2,1,3,0:T(2,128)S(1)}, f32[1,2,128,13]{2,1,3,0:T(2,128)}, u32[]{:S(2)}) copy-start(f32[1,2,128,13]{2,1,3,0:T(2,128)} %param.14) | copy-start | bytes 39940
  47.8 14.8 %copy-start.12 = (f32[13,128]{1,0:T(8,128)S(1)}, f32[13,128]{1,0:T(8,128)}, u32[]{:S(2)}) copy-start(f32[13,128]{1,0:T(8,128)} %param.16) | copy-start | bytes 19972
  47.8 14.8 %copy-start.13 = (f32[1024]{0:T(1024)S(1)}, f32[1024]{0:T(1024)}, u32[]{:S(2)}) copy-start(f32[1024]{0:T(1024)} %param.18) | copy-start | bytes 12292
  47.8 15.4 %copy-start.15 = (s32[1,2,128]{2,1,0:T(2,128)S(1)}, s32[1,2,128]{2,1,0:T(2,128)}, u32[]{:S(2)}) copy-start(s32[1,2,128]{2,1,0:T(2,128)} %param.15) | copy-start | bytes 3076
  47.8 16.4 %copy-start.14 = (s32[1,2,2,1,128]{4,3,2,1,0:T(1,128)S(1)}, s32[1,2,2,1,128]{4,3,2,1,0:T(1,128)}, u32[]{:S(2)}) copy-start(s32[1,2,2,1,128]{4,3,2,1,0:T(1,128)} %param.13) | copy-start | bytes 6148
  55.0 30.4 %all-to-all-start.2 = ((bf16[64,48,128]{2,1,0:T(8,128)(2,1)}), bf16[64,48,128]{2,1,0:T(8,128)(2,1)S(1)}, u32[]{:S(2)}, u32[]{:S(2)}) async-start(bf16[64,48,128]{2,1,0:T(8,128)(2,1)} %bitcast.7), calls=%async_computation.2 | async-start | bytes 1572864 | tf_op jit(solution)/shard_map/all_to_all | solution.py:400
  62.7 0.6 copy-start.9
  62.7 6.6 %collective-permute-start = (bf16[256,1024]{1,0:T(8,128)(2,1)S(1)}, bf16[256,1024]{1,0:T(8,128)(2,1)S(1)}, u32[]{:S(2)}, u32[]{:S(2)}) collective-permute-start(bf16[256,1024]{1,0:T(8,128)(2,1)S(1)} %bitcast.59), channel_id=1, source_target_pairs={{0,1},{1,0},{2,3},{3,2},{4,5},{5,4},{6,7},{7,6},{8,9},{9,8},{10,11... | collective-permute-start | bytes 1572872 | tf_op jit(solution)/shard_map/ppermute | solution.py:404
  68.1 1.2 copy-start
  85.4 0.8 copy-start.7
  90.2 3.6 copy-start.6
  90.2 28.8 %copy-start.8 = (f32[6,1024]{1,0:T(8,128)S(1)}, f32[6,1024]{1,0:T(8,128)}, u32[]{:S(2)}) copy-start(f32[6,1024]{1,0:T(8,128)} %param.17) | copy-start | bytes 73732
  91.6 2.0 collective-permute-start.1
  107.6 11.3 %all-to-all-start.8 = ((bf16[8,8,1024]{2,1,0:T(8,128)(2,1)}), bf16[8,8,1024]{2,1,0:T(8,128)(2,1)S(1)}, u32[]{:S(2)}, u32[]{:S(2)}) async-start(bf16[8,8,1024]{2,1,0:T(8,128)(2,1)} %bitcast.24), calls=%async_computation.8 | async-start | bytes 262144 | tf_op jit(solution)/shard_map/all_to_all | solution.py:400
  161.6 17.1 %all-to-all-start.10 = ((bf16[4,64,1024]{2,1,0:T(8,128)(2,1)}), bf16[4,64,1024]{2,1,0:T(8,128)(2,1)S(1)}, u32[]{:S(2)}, u32[]{:S(2)}) async-start(bf16[4,64,1024]{2,1,0:T(8,128)(2,1)} %broadcast_in_dim.65), calls=%async_computation.10 | async-start | bytes 1048576 | tf_op jit(solution)/shard_map/all_to_all | solution.py:400
  178.7 30.6 %all-to-all-start.6 = ((bf16[64,48,128]{2,1,0:T(8,128)(2,1)}), bf16[64,48,128]{2,1,0:T(8,128)(2,1)S(1)}, u32[]{:S(2)}, u32[]{:S(2)}) async-start(bf16[64,48,128]{2,1,0:T(8,128)(2,1)} %bitcast.18), calls=%async_computation.6 | async-start | bytes 1572864 | tf_op jit(solution)/shard_map/all_to_all | solution.py:400
  186.4 7.0 %collective-permute-start.2 = (bf16[256,1024]{1,0:T(8,128)(2,1)S(1)}, bf16[256,1024]{1,0:T(8,128)(2,1)S(1)}, u32[]{:S(2)}, u32[]{:S(2)}) collective-permute-start(bf16[256,1024]{1,0:T(8,128)(2,1)S(1)} %bitcast.61), channel_id=1, source_target_pairs={{0,1},{1,0},{2,3},{3,2},{4,5},{5,4},{6,7},{7,6},{8,9},{9,8},{10,11... | collective-permute-start | bytes 1572872 | tf_op jit(solution)/shard_map/ppermute | solution.py:404
  191.1 1.1 copy-start.1
  192.2 1.2 copy-start.3
  209.3 1.4 copy-start.2
  215.6 36.7 %copy-start.16 = (s32[16]{0:T(128)S(1)}, s32[16]{0:T(128)}, u32[]{:S(2)}) copy-start(s32[16]{0:T(128)} %param.19) | copy-start | bytes 196
  217.0 2.0 collective-permute-start.9
  242.8 29.8 %all-to-all-start.11 = ((bf16[64,48,128]{2,1,0:T(8,128)(2,1)}), bf16[64,48,128]{2,1,0:T(8,128)(2,1)S(1)}, u32[]{:S(2)}, u32[]{:S(2)}) async-start(bf16[64,48,128]{2,1,0:T(8,128)(2,1)} %bitcast.27), calls=%async_computation.11 | async-start | bytes 1572864 | tf_op jit(solution)/shard_map/all_to_all | solution.py:400
  249.5 19.2 %collective-permute-start.8 = (bf16[3072,128]{1,0:T(8,128)(2,1)S(1)}, bf16[3072,128]{1,0:T(8,128)(2,1)S(1)}, u32[]{:S(2)}, u32[]{:S(2)}) collective-permute-start(bf16[3072,128]{1,0:T(8,128)(2,1)S(1)} %bitcast.46), channel_id=1, source_target_pairs={{0,192},{64,0},{128,64},{192,128},{1,193},{65,1},{129,65},{193,129... | collective-permute-start | bytes 2359304 | tf_op jit(solution)/shard_map/ppermute | solution.py:408
  253.7 16.8 %collective-permute-start.12 = (f32[8,1024]{1,0:T(8,128)S(1)}, f32[8,1024]{1,0:T(8,128)S(1)}, u32[]{:S(2)}, u32[]{:S(2)}) collective-permute-start(f32[8,1024]{1,0:T(8,128)S(1)} %add_multiply_fusion), channel_id=1, source_target_pairs={{0,192},{64,0},{128,64},{192,128},{1,193},{65,1},{129,65},{193,129... | collective-permute-start | bytes 98312 | tf_op jit(solution)/shard_map/ppermute | solution.py:408
  254.3 35.3 %collective-permute-start.11 = (f32[8,1024]{1,0:T(8,128)S(1)}, f32[8,1024]{1,0:T(8,128)S(1)}, u32[]{:S(2)}, u32[]{:S(2)}) collective-permute-start(f32[8,1024]{1,0:T(8,128)S(1)} %add_multiply_fusion), channel_id=1, source_target_pairs={{0,64},{64,128},{128,192},{192,0},{1,65},{65,129},{129,193},{193,1... | collective-permute-start | bytes 98312 | tf_op jit(solution)/shard_map/ppermute | solution.py:408
  255.2 34.3 %collective-permute-start.10 = (f32[8,1024]{1,0:T(8,128)S(1)}, f32[8,1024]{1,0:T(8,128)S(1)}, u32[]{:S(2)}, u32[]{:S(2)}) collective-permute-start(f32[8,1024]{1,0:T(8,128)S(1)} %add_multiply_fusion), channel_id=1, source_target_pairs={{0,128},{64,192},{128,0},{192,64},{1,129},{65,193},{129,1},{193,65... | collective-permute-start | bytes 98312 | tf_op jit(solution)/shard_map/ppermute | solution.py:408
  255.7 94.1 %collective-permute-start.7 = (bf16[3072,128]{1,0:T(8,128)(2,1)S(1)}, bf16[3072,128]{1,0:T(8,128)(2,1)}, u32[]{:S(2)}, u32[]{:S(2)}) collective-permute-start(bf16[3072,128]{1,0:T(8,128)(2,1)S(1)} %bitcast.47), channel_id=1, source_target_pairs={{0,128},{64,192},{128,0},{192,64},{1,129},{65,193},{129,1},{193,65... | collective-permute-start | bytes 2359304 | tf_op jit(solution)/shard_map/ppermute | solution.py:408
  268.7 0.9 copy-start.4
  269.6 80.3 %collective-permute-start.6 = (bf16[3072,128]{1,0:T(8,128)(2,1)S(1)}, bf16[3072,128]{1,0:T(8,128)(2,1)}, u32[]{:S(2)}, u32[]{:S(2)}) collective-permute-start(bf16[3072,128]{1,0:T(8,128)(2,1)S(1)} %bitcast.48), channel_id=1, source_target_pairs={{0,64},{64,128},{128,192},{192,0},{1,65},{65,129},{129,193},{193,1... | collective-permute-start | bytes 2359304 | tf_op jit(solution)/shard_map/ppermute | solution.py:408
  272.5 112.6 %collective-permute-start.5 = (bf16[3072,128]{1,0:T(8,128)(2,1)S(1)}, bf16[3072,128]{1,0:T(8,128)(2,1)S(1)}, u32[]{:S(2)}, u32[]{:S(2)}) collective-permute-start(bf16[3072,128]{1,0:T(8,128)(2,1)S(1)} %bitcast.50), channel_id=1, source_target_pairs={{0,192},{64,0},{128,64},{192,128},{1,193},{65,1},{129,65},{193,129... | collective-permute-start | bytes 2359304 | tf_op jit(solution)/shard_map/ppermute | solution.py:408
  289.6 95.5 %collective-permute-start.4 = (bf16[3072,128]{1,0:T(8,128)(2,1)S(1)}, bf16[3072,128]{1,0:T(8,128)(2,1)}, u32[]{:S(2)}, u32[]{:S(2)}) collective-permute-start(bf16[3072,128]{1,0:T(8,128)(2,1)S(1)} %bitcast.51), channel_id=1, source_target_pairs={{0,128},{64,192},{128,0},{192,64},{1,129},{65,193},{129,1},{193,65... | collective-permute-start | bytes 2359304 | tf_op jit(solution)/shard_map/ppermute | solution.py:408
  289.6 95.5 %collective-permute-start.3 = (bf16[3072,128]{1,0:T(8,128)(2,1)S(1)}, bf16[3072,128]{1,0:T(8,128)(2,1)}, u32[]{:S(2)}, u32[]{:S(2)}) collective-permute-start(bf16[3072,128]{1,0:T(8,128)(2,1)S(1)} %bitcast.52), channel_id=1, source_target_pairs={{0,64},{64,128},{128,192},{192,0},{1,65},{65,129},{129,193},{193,1... | collective-permute-start | bytes 2359304 | tf_op jit(solution)/shard_map/ppermute | solution.py:408
  290.9 37.0 %all-to-all-start.1 = ((s32[4,64,96]{2,1,0:T(8,128)}), s32[4,64,96]{2,1,0:T(8,128)S(1)}, u32[]{:S(2)}, u32[]{:S(2)}) async-start(s32[4,64,96]{2,1,0:T(8,128)} %broadcast_in_dim.27), calls=%async_computation.1 | async-start | bytes 262144 | tf_op jit(solution)/shard_map/all_to_all | solution.py:400
  294.5 89.4 %copy-start.10 = (f32[8,1024]{1,0:T(8,128)}, f32[8,1024]{1,0:T(8,128)S(1)}, u32[]{:S(2)}) copy-start(f32[8,1024]{1,0:T(8,128)S(1)} %add_add_fusion) | copy-start | bytes 98308
  328.5 55.4 %all-to-all-start.14 = ((f32[64,1,128]{2,1,0:T(1,128)}), f32[64,1,128]{2,1,0:T(1,128)S(1)}, u32[]{:S(2)}, u32[]{:S(2)}) async-start(f32[64,1,128]{2,1,0:T(1,128)} %broadcast_in_dim.67), calls=%async_computation.14 | async-start | bytes 65536 | tf_op jit(solution)/shard_map/all_to_all | solution.py:400
  349.9 1.1 copy-start.5
where the time goes:
time: 423 us; the launch traced here: 422 us
  Pallas kernels  112 us (26%)
  starting transfers between devices  98 us (23%)
  waiting for transfers between devices  97.2 us (23%)
  blocking collectives  87.7 us (21%)
  local copies, waits for them, and re-layouts  15.5 us (4%)
  other arithmetic  9.11 us (2%)
    all_to_all x6, blocking collectives, exchange(): return lax.all_to_all(x, axis, 0, 0, tiled=True, axis_index_groups=groups)  87.7 us
    all_to_all x9, waiting for transfers between devices, exchange(): return lax.all_to_all(x, axis, 0, 0, tiled=True, axis_index_groups=groups)  83.6 us
    all_to_all x9, starting transfers between devices, exchange(): return lax.all_to_all(x, axis, 0, 0, tiled=True, axis_index_groups=groups)  70.1 us
    pallas_call x2, Pallas kernels, add_lists(): pl.pallas_call(make_total_kernel(step), name='add_lists_%d' % step, in_sp...  69.3 us
    ppermute x9, starting transfers between devices, to_group(): return lax.ppermute(x, 'group', [(i, (i + d) % NG) for i in range(NG)])  25.8 us
    pallas_call x1, Pallas kernels, owner_step(): pl.pallas_call(owner_kernel, name='owner_step', in_specs=[sm, sm, vm, hb]...  12.7 us
    ppermute x9, waiting for transfers between devices, to_group(): return lax.ppermute(x, 'group', [(i, (i + d) % NG) for i in range(NG)])  10.5 us
    pallas_call x2, Pallas kernels, dense_step(): pl.pallas_call(make_dense_kernel(step), name='dense_%d' % step, in_specs=...  8.76 us
  transfers between devices with their start and end apart: 22, of which 9 were waited for; matrix products, arithmetic and copies ran while one was open for 3% of the time, Pallas kernels for 15%

commit v1 on v0

v1 whole, which is shorter than its diff:
```python
import jax
import jax.numpy as jnp
from jax import lax
from jax.experimental import pallas as pl
from jax.experimental.pallas import tpu as pltpu
from jax.sharding import PartitionSpec as P


emb_rate = 2.0
dense_rate = 0.5
bf16 = jnp.bfloat16
f32 = jnp.float32
i32 = jnp.int32

NS = 64
NG = 4
YS = 4
CAP = 24
SLOTS = 2 * CAP
LOOKS = 512
SAMPLES = 128
EMB = 128
ROWS = 8192
HID = 1024
DENSE = 13
ALL_SLOTS = NS * SLOTS
BATCH = NS * SAMPLES


def params(mb=24):
    return pltpu.CompilerParams(vmem_limit_bytes=mb * 1024 * 1024)


vm = pl.BlockSpec(memory_space=pltpu.VMEM)
sm = pl.BlockSpec(memory_space=pltpu.SMEM)
hb = pl.BlockSpec(memory_space=pl.ANY)


def iota(shape, dim):
    return lax.broadcasted_iota(i32, shape, dim)


def ones_where(mask):
    return jnp.where(mask, 1.0, 0.0).astype(bf16)


def mm(a, b):
    return lax.dot_general(a, b, (((1,), (0,)), ((), ())), preferred_element_type=f32)


def mm_nt(a, b):
    return lax.dot_general(a, b, (((1,), (1,)), ((), ())), preferred_element_type=f32)


def mm_tn(a, b):
    return lax.dot_general(a, b, (((0,), (0,)), ((), ())), preferred_element_type=f32)


def route_kernel(me_ref, own_ref, off_ref, req_ref, slot_ref):
    earlier = ones_where(iota((LOOKS, LOOKS), 0) < iota((LOOKS, LOOKS), 1))
    total = jnp.zeros((NS, 2 * SLOTS), f32)
    count = jnp.zeros((NS, 2 * SLOTS), f32)
    for st in range(4):
        own = own_ref[st : st + 1, :]
        off = off_ref[st : st + 1, :]
        named = iota((NS, LOOKS), 0) == own
        before = mm(ones_where(named), earlier)
        rank = jnp.sum(jnp.where(named, before, 0.0), axis=0, keepdims=True).astype(i32)
        column = ones_where(iota((2 * SLOTS, LOOKS), 0) == rank + st * CAP)
        high = jnp.where(named, (off >> 8).astype(f32), 0.0).astype(bf16)
        low = jnp.where(named, (off & 255).astype(f32), 0.0).astype(bf16)
        total = total + mm_nt(high, column) * 256.0 + mm_nt(low, column)
        count = count + mm_nt(ones_where(named), column)
        slot_ref[st : st + 1, :] = own * SLOTS + (st % 2) * CAP + rank
    spare = me_ref[0] * CAP + iota((NS, 2 * SLOTS), 1) % CAP
    req_ref[...] = jnp.where(count > 0.5, total.astype(i32), spare)


def route(me, own, off):
    return pl.pallas_call(
        route_kernel,
        name="route",
        in_specs=[sm, vm, vm],
        out_specs=[vm, vm],
        out_shape=[
            jax.ShapeDtypeStruct((NS, 2 * SLOTS), i32),
            jax.ShapeDtypeStruct((4, LOOKS), i32),
        ],
        compiler_params=params(),
    )(me, own, off)


def pool_kernel(slot_ref, bag_ref, a_ref, at_ref):
    upto = ones_where(iota((SAMPLES, SAMPLES), 1) <= iota((SAMPLES, SAMPLES), 0))
    below = ones_where(iota((SAMPLES, SAMPLES), 1) < iota((SAMPLES, SAMPLES), 0))
    look = iota((SAMPLES, LOOKS), 1).astype(f32)
    for t in range(2):
        lens = jnp.broadcast_to(bag_ref[t : t + 1, :], (8, SAMPLES)).astype(f32).astype(bf16)
        ends = mm_nt(upto, lens)[:, :1]
        starts = mm_nt(below, lens)[:, :1]
        member = ones_where((look >= starts) & (look < ends))
        slot = slot_ref[t : t + 1, :]
        for q in range(ALL_SLOTS // LOOKS):
            at_slot = ones_where(iota((LOOKS, LOOKS), 0) + q * LOOKS == slot)
            a_ref[t * SAMPLES : (t + 1) * SAMPLES, q * LOOKS : (q + 1) * LOOKS] = mm_nt(
                member, at_slot
            ).astype(bf16)
            at_ref[q * LOOKS : (q + 1) * LOOKS, t * SAMPLES : (t + 1) * SAMPLES] = mm_nt(
                at_slot, member
            ).astype(bf16)


def pool_matrix(slot, bags):
    return pl.pallas_call(
        pool_kernel,
        name="pool_matrix",
        in_specs=[vm, vm],
        out_specs=[vm, vm],
        out_shape=[
            jax.ShapeDtypeStruct((2 * SAMPLES, ALL_SLOTS), bf16),
            jax.ShapeDtypeStruct((ALL_SLOTS, 2 * SAMPLES), bf16),
        ],
        compiler_params=params(),
    )(slot, bags)


def find_clashes(idx):
    lane = iota(idx.shape, 1)
    clash = jnp.zeros(idx.shape, i32)
    for d in range(1, 8):
        same = (idx == jnp.concatenate([idx[:, -d:], idx[:, :-d]], axis=1)) & (lane % 8 >= d)
        clash = clash | jnp.where(same, 1, 0)
    out = jnp.zeros(idx.shape, i32)
    for part in range(4):
        any_of = jnp.max(jnp.where(lane // CAP == part, clash, 0), axis=1, keepdims=True)
        out = jnp.where(lane == part, any_of, out)
    return out


def own_lists_kernel(idx_ref, rows_ref, flags_ref):
    idx = idx_ref[...]
    turned = idx.T
    rows_ref[...] = jnp.concatenate([turned[:SLOTS], turned[SLOTS : 2 * SLOTS]], axis=1)
    flags = find_clashes(idx).T
    flags_ref[...] = jnp.concatenate([flags[0:1] + flags[1:2], flags[2:3] + flags[3:4]], axis=1)


def all_lists_kernel(idx_ref, rows_ref, flags_ref):
    idx = idx_ref[...]
    turned = idx.T
    flags = find_clashes(idx).T
    for part in range(4):
        for half in range(2):
            cut = slice(128 * half, 128 * half + 128)
            rows_ref[part, half] = turned[part * CAP : (part + 1) * CAP, cut]
            flags_ref[part, half : half + 1] = flags[part : part + 1, cut]


def list_rows(idx, kernel, rows, flags):
    return pl.pallas_call(
        kernel,
        in_specs=[vm],
        out_specs=[vm, vm],
        out_shape=[jax.ShapeDtypeStruct(rows, i32), jax.ShapeDtypeStruct(flags, i32)],
        compiler_params=params(),
    )(jnp.pad(idx, ((0, 0), (0, 32))))


def own_lists(idx):
    return list_rows(idx, own_lists_kernel, (SLOTS, 2 * NS), (1, 2 * NS))


def all_lists(idx):
    return list_rows(idx, all_lists_kernel, (4, 2, CAP, 128), (4, 2, 128))


def gather_rows(idx_ref, first, tables, stage):
    def one(s, _):
        base = pl.multiple_of(s * SLOTS, 8)
        for j in range(SLOTS):
            row = idx_ref.at[j][first + s]
            stage[pl.ds(base + j, 1), :] = tables[j // CAP][pl.ds(row, 1), :]
        return 0

    lax.fori_loop(0, NS, one, 0)


def add_rows(lists, clear_of):
    def one(s, _):
        clear = clear_of(s)

        @pl.when(clear)
        def _():
            for b in range(0, CAP, 8):
                held = []
                for numbers, source, rows, start, table in lists:
                    base = start(s)
                    for j in range(b, b + 8):
                        row = numbers(j)[source + s]
                        held.append(
                            (table, row, table[pl.ds(row, 1), :] + rows[pl.ds(base + j, 1), :])
                        )
                for table, row, value in held:
                    table[pl.ds(row, 1), :] = value

        @pl.when(jnp.logical_not(clear))
        def _():
            for numbers, source, rows, start, table in lists:
                base = start(s)
                for j in range(CAP):
                    row = numbers(j)[source + s]
                    table[pl.ds(row, 1), :] = table[pl.ds(row, 1), :] + rows[pl.ds(base + j, 1), :]

        return 0

    lax.fori_loop(0, NS, one, 0)


def gather_kernel(idx_ref, tab_ref, out_ref, tab0, tab1, stage):
    tab0[...] = tab_ref[0].astype(f32)
    tab1[...] = tab_ref[1].astype(f32)
    gather_rows(idx_ref, 0, [tab0, tab1], stage)
    out_ref[...] = stage[...].astype(bf16)


def gather_first(idx, table):
    return pl.pallas_call(
        gather_kernel,
        name="gather_first",
        in_specs=[sm, vm],
        out_specs=vm,
        out_shape=jax.ShapeDtypeStruct((ALL_SLOTS, EMB), bf16),
        scratch_shapes=[
            pltpu.VMEM((ROWS, EMB), f32),
            pltpu.VMEM((ROWS, EMB), f32),
            pltpu.VMEM((ALL_SLOTS, EMB), f32),
        ],
        compiler_params=params(20),
    )(idx, table)


def owner_kernel(idx_ref, clash_ref, grad_ref, tab_ref, out_ref, new0, new1, stage):
    new0[...] = tab_ref[0].astype(f32)
    new1[...] = tab_ref[1].astype(f32)
    stage[...] = grad_ref[...].astype(f32) * -emb_rate
    add_rows(
        [
            (
                lambda j, t=t: idx_ref.at[t * CAP + j],
                0,
                stage,
                lambda s, t=t: pl.multiple_of(s * SLOTS + t * CAP, 8),
                new,
            )
            for t, new in enumerate((new0, new1))
        ],
        lambda s: clash_ref[0, s] == 0,
    )
    gather_rows(idx_ref, NS, [new0, new1], stage)
    out_ref[:, :SLOTS, :] = stage[...].astype(bf16).reshape(NS, SLOTS, EMB)


def owner_step(idx, clash, grads, table):
    return pl.pallas_call(
        owner_kernel,
        name="owner_step",
        in_specs=[sm, sm, vm, vm],
        out_specs=vm,
        out_shape=jax.ShapeDtypeStruct((NS, SLOTS + 32, EMB), bf16),
        scratch_shapes=[
            pltpu.VMEM((ROWS, EMB), f32),
            pltpu.VMEM((ROWS, EMB), f32),
            pltpu.VMEM((ALL_SLOTS, EMB), f32),
        ],
        compiler_params=params(20),
    )(idx, clash, grads, table)


def make_total_kernel(step, t):
    def total_kernel(me_ref, weight_ref, idx_ref, clash_ref, *refs):
        lists = refs[:NG]
        old, out_ref = (refs[NG], refs[NG + 1]) if step or t else (None, refs[NG])
        acc0, acc1, part, stage0, stage1, sems, acc_sem = refs[-7:]
        group = me_ref[1]
        apart = [(group + NG - k) % NG for k in range(NG)]

        def list_copy(d, k):
            rows = lists[d].at[:, pl.ds(0 if step else t * CAP, CAP), :]
            return pltpu.make_async_copy(rows, part.at[k], sems.at[k])

        for k in range(NG):
            for d in range(NG):

                @pl.when(apart[k] == d)
                def _(d=d, k=k):
                    list_copy(d, k).start()

        if step:
            seed = pltpu.make_async_copy(old.at[t], acc0, acc_sem)
            seed.start()
        else:
            acc0[...] = jnp.zeros(acc0.shape, f32)
        acc1[...] = jnp.zeros(acc1.shape, f32)
        for k in range(0, NG, 2):
            for i, stage in enumerate((stage0, stage1)):
                list_copy(0, k + i).wait()
                stage[...] = part[k + i].reshape(NS * CAP, EMB).astype(f32) * weight_ref[k + i]
            if step and k == 0:
                seed.wait()
            halves = [apart[k + i] // 2 for i in range(2)]
            sources = [(apart[k + i] % 2) * NS for i in range(2)]
            add_rows(
                [
                    (
                        lambda j, i=i: idx_ref.at[halves[i], j],
                        sources[i],
                        (stage0, stage1)[i],
                        lambda s: pl.multiple_of(s * CAP, 8),
                        (acc0, acc1)[i],
                    )
                    for i in range(2)
                ],
                lambda s: clash_ref.at[halves[0]][sources[0] + s]
                + clash_ref.at[halves[1]][sources[1] + s]
                == 0,
            )
        acc0[...] = acc0[...] + acc1[...]
        result = pltpu.make_async_copy(acc0, out_ref.at[t], acc_sem)
        result.start()
        result.wait()

    return total_kernel


def add_lists(me, weights, idx, clash, lists, old, step, t):
    part = 2 * step + t
    operands = [me, weights, idx[part], clash[part], *lists] + ([old] if step or t else [])
    return pl.pallas_call(
        make_total_kernel(step, t),
        in_specs=[sm, sm, sm, sm] + [hb] * (len(operands) - 4),
        out_specs=hb,
        out_shape=jax.ShapeDtypeStruct((2, ROWS, EMB), f32),
        input_output_aliases={4 + NG: 0} if step or t else {},
        scratch_shapes=[
            pltpu.VMEM((ROWS, EMB), f32),
            pltpu.VMEM((ROWS, EMB), f32),
            pltpu.VMEM((NG, NS, CAP, EMB), bf16),
            pltpu.VMEM((NS * CAP, EMB), f32),
            pltpu.VMEM((NS * CAP, EMB), f32),
            pltpu.SemaphoreType.DMA((NG,)),
            pltpu.SemaphoreType.DMA,
        ],
        compiler_params=params(16),
    )(*operands)


def block_device(me, other):
    row = iota((384, 256), 1)
    return (2 * (row // 8) + other) ^ me, row % 8


def top_pick(me, other):
    device, inside = block_device(me, other)
    return ones_where((inside < 6) & (device * 6 + inside == iota((384, 256), 0)))


def rest_pick(me, other):
    device, inside = block_device(me, other)
    return ones_where((inside == 6) & (device == iota((384, 256), 0)))[:32]


def piece_picks(b):
    row = iota((384, NS * 16), 1)
    want = iota((384, NS * 16), 0)
    inside = row % 16 - 8 * b
    top = (inside >= 0) & (inside < 6) & ((row // 16) * 6 + inside == want)
    rest = (inside == 6) & (row // 16 == want)
    return ones_where(top), ones_where(rest)[:32]


def sigmoid(v):
    return 1.0 / (1.0 + jnp.exp(-v))


def make_dense_kernel(step):
    def dense_kernel(
        me_ref, a_ref, at_ref, feat_ref, lab_ref, wa_ref, wb_ref, *refs
    ):
        refs = list(refs)
        me = me_ref[0]
        if step:
            core = me % 2
            halves = []
            rests = []
            for part in (wa_ref[:, SLOTS:, :], wb_ref[...]):
                tiles = [part[:, 16 * u : 16 * u + 16, :].reshape(NS * 16, EMB) for u in range(2)]
                picks = [piece_picks(b) for b in range(2)]
                halves.append(
                    jnp.concatenate([mm(picks[j % 2][0], tiles[j // 2]) for j in range(4)], axis=1)
                )
                rests.append(sum(mm(picks[j % 2][1], tiles[j // 2]) for j in range(3)))
            w = jnp.concatenate(
                [
                    jnp.where(core == 0, halves[0], halves[1]),
                    jnp.where(core == 0, halves[1], halves[0]),
                ],
                axis=1,
            ).astype(bf16)
            rest = jnp.where(core == 0, rests[0], rests[1])
            rep = wa_ref[:, :SLOTS, :].reshape(ALL_SLOTS, EMB)
        else:
            w = (mm(top_pick(me, 0), wa_ref[...]) + mm(top_pick(me, 1), wb_ref[...])).astype(bf16)
            rest = refs.pop(0)[...]
            rep = refs.pop(0)[...]
        hold_ref, joined_ref, dpre_ref, grad_ref = refs
        out_row = jnp.concatenate([rest[DENSE + k : DENSE + k + 1, :] for k in range(8)], axis=1)
        feats = feat_ref[...]
        bpre = jnp.zeros((SAMPLES, EMB), f32)
        for k in range(DENSE):
            bpre = bpre + feats[:, k : k + 1] * rest[k : k + 1, :]
        bgate = sigmoid(bpre)
        bottom = bpre * bgate
        pooled = mm(a_ref[...], rep)
        joined = jnp.concatenate([bottom, pooled[:SAMPLES], pooled[SAMPLES:]], axis=1).astype(bf16)
        pre = mm(joined, w)
        gate = sigmoid(pre)
        hidden = pre * gate
        logit = jnp.sum(hidden * out_row, axis=1, keepdims=True)
        dlogit = sigmoid(logit) - lab_ref[...]
        dpre = (dlogit * out_row * (gate * (1.0 + pre * (1.0 - gate)))).astype(bf16)
        dz = mm_nt(dpre, w)
        both = jnp.concatenate([dz[:, EMB : 2 * EMB], dz[:, 2 * EMB :]], axis=0).astype(bf16)
        hold_ref[...] = mm(at_ref[...], both).astype(bf16)
        joined_ref[...] = joined
        dpre_ref[...] = dpre
        dbottom = dz[:, :EMB] * (bgate * (1.0 + bpre * (1.0 - bgate)))
        for k in range(DENSE):
            grad_ref[k : k + 1, :] = jnp.sum(feats[:, k : k + 1] * dbottom, axis=0, keepdims=True)
        dout = jnp.sum(hidden * dlogit, axis=0, keepdims=True)
        for k in range(8):
            grad_ref[DENSE + k : DENSE + k + 1, :] = dout[:, k * EMB : (k + 1) * EMB]
        grad_ref[DENSE + 8 :, :] = jnp.zeros((32 - DENSE - 8, EMB), f32)

    return dense_kernel


def dense_step(me, a, at, feats, labels, more, step):
    operands = [me, a, at, feats, labels, *more]
    return pl.pallas_call(
        make_dense_kernel(step),
        in_specs=[sm] + [vm] * (len(operands) - 1),
        out_specs=[vm] * 4,
        out_shape=[
            jax.ShapeDtypeStruct((ALL_SLOTS, EMB), bf16),
            jax.ShapeDtypeStruct((SAMPLES, 384), bf16),
            jax.ShapeDtypeStruct((SAMPLES, HID), bf16),
            jax.ShapeDtypeStruct((32, EMB), f32),
        ],
        compiler_params=params(),
    )(*operands)


def weight_grad_kernel(me_ref, joined_ref, dpre_ref, rest_ref, keep_ref, send_ref):
    me = me_ref[0]
    joined = joined_ref[...]
    dpre = dpre_ref[...]
    rest = rest_ref[...].astype(bf16)
    for which, out in ((0, keep_ref), (1, send_ref)):
        picked = mm(joined, top_pick(me, which)).astype(bf16)
        out[...] = mm_tn(picked, dpre).astype(out.dtype)
        more = mm_tn(rest_pick(me, which), rest)
        out[:, :EMB] = (out[:, :EMB].astype(f32) + more).astype(out.dtype)


def weight_grad(me, joined, dpre, rest):
    return pl.pallas_call(
        weight_grad_kernel,
        name="weight_grad",
        in_specs=[sm, vm, vm, vm],
        out_specs=[vm, vm],
        out_shape=[
            jax.ShapeDtypeStruct((256, HID), f32),
            jax.ShapeDtypeStruct((256, HID), bf16),
        ],
        compiler_params=params(),
    )(me, joined, dpre, rest)


def exchange(x):
    return lax.all_to_all(x, "shard", 0, 0, tiled=True)


def to_group(x, d):
    return lax.ppermute(x, "group", [(i, (i + d) % NG) for i in range(NG)])


def from_groups(x):
    return [x] + [to_group(x, d) for d in range(1, NG)]


def swap(x, bits):
    return lax.ppermute(x, "shard", [(i, i ^ bits) for i in range(NS)])


def spread(block):
    have = block
    for bits in (2, 4, 8):
        have = jnp.concatenate([have, swap(have, bits)], 0)
    have = jnp.concatenate([have] + [swap(have, 16 * d) for d in range(1, YS)], 0)
    return have, swap(have, 1)


def summed(keep, send):
    half = keep + swap(send, 1).astype(f32)
    low = half[64:].astype(bf16)
    got = [swap(low[64 * d - 64 : 64 * d], 16 * d).astype(f32) for d in range(1, YS)]
    half = half[:64] + got[0] + got[1] + got[2]
    half = half[:32] + swap(half[32:].astype(bf16), 8).astype(f32)
    got = [swap(half[8 * d : 8 * d + 8], 2 * d) for d in range(1, 4)]
    return half[:8] + got[0] + got[1] + got[2]


def in_three(v):
    a = lax.reduce_precision(v, 8, 7)
    b = lax.reduce_precision(v - a, 8, 7)
    c = v - a - b
    return a, b, c


def whole_round(
    table,
    owners,
    offsets,
    bag_lengths,
    dense_feats,
    labels,
    bottom_weight,
    top_weight,
    out_weight,
    client_group,
):
    shard = lax.axis_index("shard")
    group = lax.axis_index("group")
    me = jnp.stack([shard, group]).astype(i32)
    counts = jnp.sum((client_group[None, :] == jnp.arange(NG)[:, None]).astype(f32), axis=1)
    weights = counts * NG / client_group.shape[0]
    requests, slots = route(me, owners.reshape(4, LOOKS), offsets.reshape(4, LOOKS))
    rest = jnp.concatenate(
        [bottom_weight, out_weight.reshape(8, EMB), jnp.zeros((NS - DENSE - 8, EMB), f32)], 0
    )
    my_rest = lax.dynamic_slice_in_dim(rest, shard, 1, 0)
    received = exchange(requests)
    idx_all = jnp.concatenate(from_groups(received), 0)
    first_blocks = spread(jnp.pad(top_weight, ((0, 2), (0, 0))).astype(bf16))
    matrices = []
    for s in range(2):
        matrices.append(pool_matrix(slots[2 * s : 2 * s + 2], bag_lengths[0, s, :, 0]))
    own_idx, own_clash = own_lists(received)
    all_idx, all_clash = all_lists(idx_all)
    served = gather_first(own_idx, table).reshape(NS, SLOTS, EMB)
    total = None
    top_sum = jnp.zeros((8, HID), f32)
    for step in range(2):
        replies = exchange(served)
        if step:
            more = [replies, swap(replies[:, SLOTS:], 1)]
        else:
            more = [*first_blocks, rest[:32], replies.reshape(ALL_SLOTS, EMB)]
        hold, joined, dpre, rest_grad = dense_step(
            me,
            *matrices[step],
            dense_feats[0, step],
            labels[0, step].astype(f32)[:, None],
            more,
            step,
        )
        grads = exchange(hold.reshape(NS, SLOTS, EMB))
        parts = weight_grad(me, joined, dpre, rest_grad)
        top_grad = summed(*parts)
        top_sum = top_sum + top_grad
        if step == 0:
            served = owner_step(own_idx, own_clash, grads.reshape(ALL_SLOTS, EMB), table)
            new = jnp.pad(top_weight, ((0, 2), (0, 0))) - dense_rate * (top_grad / BATCH)
            parts = in_three(my_rest - dense_rate * (top_grad[6:7, :EMB] / BATCH))
            row = jnp.concatenate([*parts, jnp.zeros((1, HID - 3 * EMB), f32)], 1)
            block = jnp.concatenate([new[:6], row, jnp.zeros((1, HID), f32)], 0).astype(bf16)
            tiles = jnp.concatenate([block[:, EMB * j : EMB * (j + 1)] for j in range(8)], 0)
            tiles = jnp.broadcast_to(tiles.reshape(1, 2, 32, EMB), (NS // 2, 2, 32, EMB))
            served = served.at[:, SLOTS:, :].set(tiles.reshape(NS, 32, EMB))
            lists = from_groups(grads)
            for t in range(2):
                total = add_lists(me, -emb_rate * weights, all_idx, all_clash, lists, total, 0, t)
        else:
            for t in range(2):
                lists = from_groups(grads[:, t * CAP : (t + 1) * CAP])
                total = add_lists(me, -emb_rate * weights, all_idx, all_clash, lists, total, 1, t)
    mine = weights[group] * (-dense_rate / BATCH) * top_sum
    a, b, c, d = from_groups(mine)
    dense = (a + c) + (b + d)
    ends = exchange(jnp.broadcast_to(dense[6:7, :EMB][None], (NS, 1, EMB))).reshape(NS, EMB)
    return (
        total,
        dense[:6],
        ends[:DENSE],
        ends[DENSE : DENSE + 8].reshape(HID),
    )


def solution(mesh):
    in_specs = (
        P(None, "shard", None),
        P("group", None, None, "shard", None),
        P("group", None, None, "shard"),
        P("group", None, None, "shard", None),
        P("group", None, "shard", None),
        P("group", None, "shard"),
        P(),
        P("shard", None),
        P(),
        P(),
    )
    out_specs = (P(None, "shard", None), P("shard", None), P(), P())
    return jax.shard_map(whole_round, mesh=mesh, in_specs=in_specs, out_specs=out_specs, check_vma=False)
```

time: 423 us -> 397 us (0.939); the launches traced: 422 us -> 390 us
  blocking collectives: 87.7 us -> 40.2 us
  waiting for transfers between devices: 97.2 us -> 114 us
  Pallas kernels: 112 us -> 95.3 us
  local copies, waits for them, and re-layouts: 15.5 us -> 25.3 us
  starting transfers between devices: 98 us -> 107 us
    all_to_all x9 -> x5, waiting for transfers between devices: 83.6 us -> 26.6 us  [exchange(): return lax.all_to_all(x, 'shard', 0, 0, tiled=True)]
    ppermute x4 -> x24, waiting for transfers between devices: 3.08 us -> 56 us  [swap(): return lax.ppermute(x, 'shard', [(i, i ^ bits) for i in range(NS)])]
    all_to_all x6 -> x1, blocking collectives: 87.7 us -> 40.2 us  [exchange(): return lax.all_to_all(x, 'shard', 0, 0, tiled=True)]
    ppermute x4 -> x24, starting transfers between devices: 2 us -> 37.4 us  [swap(): return lax.ppermute(x, 'shard', [(i, i ^ bits) for i in range(NS)])]
    ppermute x9 -> x15, waiting for transfers between devices: 10.5 us -> 31.8 us  [to_group(): return lax.ppermute(x, 'group', [(i, (i + d) % NG) for i in range(NG)])]
    all_to_all x9 -> x5, starting transfers between devices: 70.1 us -> 50.8 us  [exchange(): return lax.all_to_all(x, 'shard', 0, 0, tiled=True)]
    pallas_call x7 -> x9, Pallas kernels: 92 us -> 77.6 us  [the longest x4 59.9 us: add_lists(): pl.pallas_call(make_total_kernel(step, t), in_specs=[sm, sm, sm, sm] + [h...]
    ppermute x9 -> x15, starting transfers between devices: 25.8 us -> 18.5 us  [to_group(): return lax.ppermute(x, 'group', [(i, (i + d) % NG) for i in range(NG)])]
  transfers between devices with their start and end apart: 22 -> 44, of which waited for: 9 -> 16; matrix products, arithmetic and copies ran while one was open for 3% -> 4% of each run, Pallas kernels for 15% -> 15%
where the time goes in v1:
time: 397 us; the launch traced here: 390 us
  waiting for transfers between devices  114 us (29%)
  starting transfers between devices  107 us (27%)
  Pallas kernels  95.3 us (24%)
  blocking collectives  40.2 us (10%)
  local copies, waits for them, and re-layouts  25.3 us (6%)
  other arithmetic  6.07 us (2%)
    pallas_call x4, Pallas kernels, add_lists(): pl.pallas_call(make_total_kernel(step, t), in_specs=[sm, sm, sm, sm] + [h...  59.9 us
    ppermute x24, waiting for transfers between devices, swap(): return lax.ppermute(x, 'shard', [(i, i ^ bits) for i in range(NS)])  56 us
    all_to_all x5, starting transfers between devices, exchange(): return lax.all_to_all(x, 'shard', 0, 0, tiled=True)  50.8 us
    all_to_all x1, blocking collectives, exchange(): return lax.all_to_all(x, 'shard', 0, 0, tiled=True)  40.2 us
    ppermute x24, starting transfers between devices, swap(): return lax.ppermute(x, 'shard', [(i, i ^ bits) for i in range(NS)])  37.4 us
    ppermute x15, waiting for transfers between devices, to_group(): return lax.ppermute(x, 'group', [(i, (i + d) % NG) for i in range(NG)])  31.8 us
    all_to_all x5, waiting for transfers between devices, exchange(): return lax.all_to_all(x, 'shard', 0, 0, tiled=True)  26.6 us
    ppermute x15, starting transfers between devices, to_group(): return lax.ppermute(x, 'group', [(i, (i + d) % NG) for i in range(NG)])  18.5 us
  transfers between devices with their start and end apart: 44, of which 16 were waited for; matrix products, arithmetic and copies ran while one was open for 4% of the time, Pallas kernels for 15%

profile of v1, /device:TPU:1, one launch (start us, length us, event | category | flops | bytes accessed | tf_op | source)
XLA Modules:
  0.0 390.0 jit_solution(12572836309347685361)
XLA Ops:
  1.4 2.5 collective-permute-start.3
  5.4 2.5 route.1
  8.4 11.7 %all-to-all-start = ((s32[64,1,96]{2,1,0:T(1,128)}), s32[64,1,96]{2,1,0:T(1,128)S(1)}, u32[]{:S(2)}, u32[]{:S(2)}) async-start(s32[64,1,96]{2,1,0:T(1,128)} %bitcast.3), calls=%async_computation | async-start | bytes 65536 | tf_op jit(solution)/shard_map/all_to_all | solution.py:490
  21.0 2.3 collective-permute-start.4
  23.4 1.4 fusion.21
  24.8 4.7 %all-to-all-done = s32[64,1,96]{2,1,0:T(1,128)S(1)} async-done(((s32[64,1,96]{2,1,0:T(1,128)}), s32[64,1,96]{2,1,0:T(1,128)S(1)}, u32[]{:S(2)}, u32[]{:S(2)}) %all-to-all-start) | async-done | bytes 24608 | tf_op jit(solution)/shard_map/all_to_all | solution.py:490
  30.5 2.2 copy-done
  32.6 4.4 %gather_first.1 = bf16[3072,128]{1,0:T(8,128)(2,1)} custom-call(s32[48,128]{1,0:T(8,128)S(1)} %get-tuple-element.44.idx_ref, bf16[2,8192,128]{2,1,0:T(8,128)(2,1)S(1)} %copy-done), custom_call_target="tpu_custom_call" | custom-call | tf_op jit(solution)/shard_map/gather_first/pallas_call | solution.py:227
  37.1 4.8 %all-to-all-start.1 = ((bf16[64,48,128]{2,1,0:T(8,128)(2,1)}), bf16[64,48,128]{2,1,0:T(8,128)(2,1)S(1)}, u32[]{:S(2)}, u32[]{:S(2)}) async-start(bf16[64,48,128]{2,1,0:T(8,128)(2,1)} %bitcast.15), calls=%async_computation.1 | async-start | bytes 1572864 | tf_op jit(solution)/shard_map/all_to_all | solution.py:490
  41.9 5.4 %collective-permute-start.5 = (bf16[32,1024]{1,0:T(8,128)(2,1)S(1)}, bf16[32,1024]{1,0:T(8,128)(2,1)S(1)}, u32[]{:S(2)}, u32[]{:S(2)}) collective-permute-start(bf16[32,1024]{1,0:T(8,128)(2,1)S(1)} %pad_maximum_fusion.1), channel_id=1, source_target_pairs={{0,8},{1,9},{2,10},{3,11},{4,12},{5,13},{6,14},{7,15},{8,0},{9,1},... | collective-permute-start | bytes 196616 | tf_op jit(solution)/shard_map/ppermute | solution.py:502
  47.3 18.8 %collective-permute-done.5 = bf16[32,1024]{1,0:T(8,128)(2,1)S(1)} collective-permute-done((bf16[32,1024]{1,0:T(8,128)(2,1)S(1)}, bf16[32,1024]{1,0:T(8,128)(2,1)S(1)}, u32[]{:S(2)}, u32[]{:S(2)}) %collective-permute-start.5) | collective-permute-done | bytes 65568 | tf_op jit(solution)/shard_map/ppermute | solution.py:502
  66.1 1.4 collective-permute-start.6
  67.5 2.6 collective-permute-start.7
  70.2 5.6 %collective-permute-done.7 = bf16[64,1024]{1,0:T(8,128)(2,1)S(1)} collective-permute-done((bf16[64,1024]{1,0:T(8,128)(2,1)S(1)}, bf16[64,1024]{1,0:T(8,128)(2,1)S(1)}, u32[]{:S(2)}, u32[]{:S(2)}) %collective-permute-start.7) | collective-permute-done | bytes 131104 | tf_op jit(solution)/shard_map/ppermute | solution.py:502
  75.8 2.6 collective-permute-done.8
  78.4 1.4 collective-permute-start.9
  81.7 3.9 %pool_matrix.3 = (bf16[256,3072]{1,0:T(8,128)(2,1)S(1)}, bf16[3072,256]{1,0:T(8,128)(2,1)S(1)}) custom-call(s32[2,512]{1,0:T(2,128)S(1)} %get-tuple-element.88.slot_ref, s32[2,128]{1,0:T(2,128)S(1)} %get-tuple-element.94.bag_ref), custom_call_target="tpu_custom_call" | custom-call | tf_op jit(solution)/shard_map/pool_matrix/pallas_call | solution.py:114
  85.7 1.1 copy-done.2
  86.8 1.4 copy-done.3
  88.9 3.9 %shard_map.131 = (bf16[3072,128]{1,0:T(8,128)(2,1)}, bf16[128,384]{1,0:T(8,128)(2,1)S(1)}, bf16[128,1024]{1,0:T(8,128)(2,1)S(1)}, f32[32,128]{1,0:T(8,128)S(1)}) custom-call(s32[2]{0:T(128)S(1)} %copy-done.15, bf16[256,3072]{1,0:T(8,128)(2,1)S(1)} %get-tuple-element.46.a_ref, bf16[3072,256]{1,0:T(8,128)(2,1)S(1)} %copy-done.3, f32[128,13]{1,0:T(8,128)S(1)} %bitcast.52, ...), custom_call_target="tpu_custom_call" | custom-call | tf_op jit(solution)/shard_map/pallas_call | solution.py:449
  92.8 1.4 weight_grad.2
  94.3 1.9 collective-permute-done.10
  96.5 1.3 collective-permute-start.12
  97.8 2.5 collective-permute-start.13
  101.4 2.7 collective-permute-done.12
  104.1 2.5 collective-permute-done.13
  106.9 7.1 %collective-permute-done.14 = bf16[32,1024]{1,0:T(8,128)(2,1)S(1)} collective-permute-done((bf16[32,1024]{1,0:T(8,128)(2,1)S(1)}, bf16[32,1024]{1,0:T(8,128)(2,1)S(1)}, u32[]{:S(2)}, u32[]{:S(2)}) %collective-permute-start.14) | collective-permute-done | bytes 65568 | tf_op jit(solution)/shard_map/ppermute | solution.py:502
  114.0 2.1 collective-permute-start.15
  116.1 2.2 collective-permute-start.17
  118.4 8.4 %all-to-all-start.2 = ((bf16[64,48,128]{2,1,0:T(8,128)(2,1)}), bf16[64,48,128]{2,1,0:T(8,128)(2,1)S(1)}, u32[]{:S(2)}, u32[]{:S(2)}) async-start(bf16[64,48,128]{2,1,0:T(8,128)(2,1)} %bitcast.17), calls=%async_computation.2 | async-start | bytes 1572864 | tf_op jit(solution)/shard_map/all_to_all | solution.py:490
  127.7 21.9 %all-to-all-done.2.refs_0_ = bf16[64,48,128]{2,1,0:T(8,128)(2,1)S(1)} async-done(((bf16[64,48,128]{2,1,0:T(8,128)(2,1)}), bf16[64,48,128]{2,1,0:T(8,128)(2,1)S(1)}, u32[]{:S(2)}, u32[]{:S(2)}) %all-to-all-start.2) | async-done | bytes 786464 | tf_op jit(solution)/shard_map/all_to_all | solution.py:490
  149.6 2.2 copy-done.1
  151.8 7.1 %owner_step.1 = bf16[64,80,128]{2,1,0:T(8,128)(2,1)S(1)} custom-call(s32[48,128]{1,0:T(8,128)S(1)} %copy-done.7, s32[1,128]{1,0:T(1,128)S(1)} %copy-done.21, bf16[3072,128]{1,0:T(8,128)(2,1)S(1)} %bitcast.50, bf16[2,8192,128]{2,1,0:T(8,128)(2,1)S(1)} %copy-done.1), custom_call_target="tpu_custom_call" | custom-call | tf_op jit(solution)/shard_map/owner_step/pallas_call | solution.py:264
  159.2 40.2 %all_to_all.37.wa_ref = bf16[64,80,128]{2,1,0:T(8,128)(2,1)S(1)} all-to-all(bf16[64,80,128]{2,1,0:T(8,128)(2,1)S(1)} %constant_dynamic-update-slice_fusion.15), channel_id=1, replica_groups=mesh['group'=4,'shard'=64] {'shard'}, dimensions={0} | all-to-all | bytes 2621440 | tf_op jit(solution)/shard_map/all_to_all | solution.py:490
  199.7 4.0 %pool_matrix.2 = (bf16[256,3072]{1,0:T(8,128)(2,1)S(1)}, bf16[3072,256]{1,0:T(8,128)(2,1)S(1)}) custom-call(s32[2,512]{1,0:T(2,128)S(1)} %copy-done.17, s32[2,128]{1,0:T(2,128)S(1)} %copy-done.19), custom_call_target="tpu_custom_call" | custom-call | tf_op jit(solution)/shard_map/pool_matrix/pallas_call | solution.py:114
  203.7 5.4 %shard_map.132 = (bf16[3072,128]{1,0:T(8,128)(2,1)}, bf16[128,384]{1,0:T(8,128)(2,1)S(1)}, bf16[128,1024]{1,0:T(8,128)(2,1)S(1)}, f32[32,128]{1,0:T(8,128)S(1)}) custom-call(s32[2]{0:T(128)S(1)} %copy-done.16, bf16[256,3072]{1,0:T(8,128)(2,1)S(1)} %get-tuple-element.42.a_ref, bf16[3072,256]{1,0:T(8,128)(2,1)S(1)} %get-tuple-element.43.at_ref, ...), custom_call_target="tpu_custom_call" | custom-call | tf_op jit(solution)/shard_map/pallas_call | solution.py:449
  209.1 1.4 weight_grad.3
  211.2 6.3 %all-to-all-start.4 = ((bf16[64,48,128]{2,1,0:T(8,128)(2,1)}), bf16[64,48,128]{2,1,0:T(8,128)(2,1)}, u32[]{:S(2)}, u32[]{:S(2)}) async-start(bf16[64,48,128]{2,1,0:T(8,128)(2,1)} %bitcast.21), calls=%async_computation.4 | async-start | bytes 1572864 | tf_op jit(solution)/shard_map/all_to_all | solution.py:490
  217.5 1.3 fusion.13
  218.9 1.6 collective-permute-start.29
  220.5 2.6 collective-permute-start.30
  223.2 2.5 collective-permute-done.29
  225.7 8.2 %collective-permute-done.30 = bf16[64,1024]{1,0:T(8,128)(2,1)S(1)} collective-permute-done((bf16[64,1024]{1,0:T(8,128)(2,1)S(1)}, bf16[64,1024]{1,0:T(8,128)(2,1)S(1)}, u32[]{:S(2)}, u32[]{:S(2)}) %collective-permute-start.30) | collective-permute-done | bytes 131104 | tf_op jit(solution)/shard_map/ppermute | solution.py:502
  233.9 3.0 collective-permute-done.31
  236.9 4.8 %collective-permute-start.32 = (bf16[32,1024]{1,0:T(8,128)(2,1)S(1)}, bf16[32,1024]{1,0:T(8,128)(2,1)S(1)}, u32[]{:S(2)}, u32[]{:S(2)}) collective-permute-start(bf16[32,1024]{1,0:T(8,128)(2,1)S(1)} %slice.351), channel_id=1, source_target_pairs={{0,8},{1,9},{2,10},{3,11},{4,12},{5,13},{6,14},{7,15},{8,0},{9,1},... | collective-permute-start | bytes 196616 | tf_op jit(solution)/shard_map/ppermute | solution.py:502
  242.9 1.3 collective-permute-start
  244.2 2.4 collective-permute-start.1
  246.7 1.2 collective-permute-start.2
  249.6 1.9 collective-permute-start.35
  253.9 1.6 collective-permute-start.26
  257.0 2.3 collective-permute-start.36
  259.3 2.0 fusion.16
  261.3 27.0 %collective-permute-done.36 = f32[8,1024]{1,0:T(8,128)} collective-permute-done((f32[8,1024]{1,0:T(8,128)}, f32[8,1024]{1,0:T(8,128)}, u32[]{:S(2)}, u32[]{:S(2)}) %collective-permute-start.36) | collective-permute-done | bytes 32800 | tf_op jit(solution)/shard_map/ppermute | solution.py:494
  288.3 2.9 collective-permute-start.38
  293.3 1.4 collective-permute-start.23
  294.7 1.9 collective-permute-start.24
  297.2 1.8 collective-permute-start.20
  299.0 4.1 %collective-permute-done.22.refs_1_ = bf16[64,24,128]{2,1,0:T(8,128)(2,1)S(1)} collective-permute-done((bf16[64,24,128]{2,1,0:T(8,128)(2,1)}, bf16[64,24,128]{2,1,0:T(8,128)(2,1)S(1)}, u32[]{:S(2)}, u32[]{:S(2)}) %collective-permute-start.22) | collective-permute-done | bytes 393248 | tf_op jit(solution)/shard_map/ppermute | solution.py:494
  304.5 19.5 %all-to-all-start.5 = ((f32[64,1,128]{2,1,0:T(1,128)}), f32[64,1,128]{2,1,0:T(1,128)}, u32[]{:S(2)}, u32[]{:S(2)}) async-start(f32[64,1,128]{2,1,0:T(1,128)} %broadcast_in_dim.34), calls=%async_computation.5 | async-start | bytes 65536 | tf_op jit(solution)/shard_map/all_to_all | solution.py:490
  325.5 14.2 %shard_map.133.refs_4_ = f32[2,8192,128]{2,1,0:T(8,128)} custom-call(s32[2]{0:T(128)S(1)} %copy-done.16, f32[4]{0:T(128)S(1)} %get-tuple-element.99.weight_ref, s32[2,24,128]{2,1,0:T(8,128)S(1)} %copy-done.12, s32[2,128]{1,0:T(2,128)S(1)} %get-tuple-element.90.clash_ref, bf16[64,48,128]{2,1,0:T(8,128)(2,1)S(1)} %all-to-all-done.2.refs_0_, ...), custom_call_target="tpu_custom_call" | custom-call | tf_op jit(solution)/shard_map/pallas_call | solution.py:338
  339.7 14.0 %shard_map.134.refs_4_ = f32[2,8192,128]{2,1,0:T(8,128)} custom-call(s32[2]{0:T(128)S(1)} %copy-done.16, f32[4]{0:T(128)S(1)} %get-tuple-element.99.weight_ref, s32[2,24,128]{2,1,0:T(8,128)S(1)} %copy-done.13, s32[2,128]{1,0:T(2,128)S(1)} %get-tuple-element.91.clash_ref, ...), custom_call_target="tpu_custom_call", output_to_operand_aliasing={{}: (8, {})} | custom-call | tf_op jit(solution)/shard_map/pallas_call | solution.py:338
  355.0 1.3 slice.295
  358.0 15.8 %shard_map.135.refs_4_ = f32[2,8192,128]{2,1,0:T(8,128)} custom-call(s32[2]{0:T(128)S(1)} %copy-done.16, f32[4]{0:T(128)S(1)} %get-tuple-element.99.weight_ref, s32[2,24,128]{2,1,0:T(8,128)S(1)} %copy-done.9, s32[2,128]{1,0:T(2,128)S(1)} %get-tuple-element.92.clash_ref, ...), custom_call_target="tpu_custom_call", output_to_operand_aliasing={{}: (8, {})} | custom-call | tf_op jit(solution)/shard_map/pallas_call | solution.py:338
  373.9 15.9 %shard_map.136 = f32[2,8192,128]{2,1,0:T(8,128)} custom-call(s32[2]{0:T(128)S(1)} %copy-done.16, f32[4]{0:T(128)S(1)} %get-tuple-element.99.weight_ref, s32[2,24,128]{2,1,0:T(8,128)S(1)} %copy-done.8, s32[2,128]{1,0:T(2,128)S(1)} %get-tuple-element.93.clash_ref, bf16[64,24,128]{2,1,0:T(8,128)(2,1)S(1)} %get-tuple-element.69.refs_0_, ...), custom_call_target="tpu_custom_call", output_to_operand_aliasing={{}: (8, {})} | custom-call | tf_op jit(solution)/shard_map/pallas_call | solution.py:338
  (176 shorter events, 26.0 us)
Async XLA Ops:
  1.4 19.6 %collective-permute-start.3 = (bf16[8,1024]{1,0:T(8,128)(2,1)S(1)}, bf16[8,1024]{1,0:T(8,128)(2,1)S(1)}, u32[]{:S(2)}, u32[]{:S(2)}) collective-permute-start(bf16[8,1024]{1,0:T(8,128)(2,1)S(1)} %get-tuple-element.67), channel_id=1, source_target_pairs={{0,2},{1,3},{2,0},{3,1},{4,6},{5,7},{6,4},{7,5},{8,10},{9,11},{10,... | collective-permute-start | bytes 49160 | tf_op jit(solution)/shard_map/ppermute | solution.py:502
  8.4 21.0 %all-to-all-start = ((s32[64,1,96]{2,1,0:T(1,128)}), s32[64,1,96]{2,1,0:T(1,128)S(1)}, u32[]{:S(2)}, u32[]{:S(2)}) async-start(s32[64,1,96]{2,1,0:T(1,128)} %bitcast.3), calls=%async_computation | async-start | bytes 65536 | tf_op jit(solution)/shard_map/all_to_all | solution.py:490
  21.0 59.5 %copy-start.25 = (f32[64,128]{1,0:T(8,128)}, f32[64,128]{1,0:T(8,128)S(1)}, u32[]{:S(2)}) copy-start(f32[64,128]{1,0:T(8,128)S(1)} %maximum_maximum_fusion) | copy-start | bytes 98308
  21.0 20.9 %collective-permute-start.4 = (bf16[16,1024]{1,0:T(8,128)(2,1)S(1)}, bf16[16,1024]{1,0:T(8,128)(2,1)S(1)}, u32[]{:S(2)}, u32[]{:S(2)}) collective-permute-start(bf16[16,1024]{1,0:T(8,128)(2,1)S(1)} %pad_maximum_fusion.2), channel_id=1, source_target_pairs={{0,4},{1,5},{2,6},{3,7},{4,0},{5,1},{6,2},{7,3},{8,12},{9,13},{10,... | collective-permute-start | bytes 98312 | tf_op jit(solution)/shard_map/ppermute | solution.py:502
  29.5 7.6 %copy-start.22 = (s32[64,1,96]{2,1,0:T(1,128)}, s32[64,1,96]{2,1,0:T(1,128)S(1)}, u32[]{:S(2)}) copy-start(s32[64,1,96]{2,1,0:T(1,128)S(1)} %all-to-all-done) | copy-start | bytes 73732
  30.4 6.6 %copy-start.6 = (s32[48,128]{1,0:T(8,128)}, s32[48,128]{1,0:T(8,128)S(1)}, u32[]{:S(2)}) copy-start(s32[48,128]{1,0:T(8,128)S(1)} %get-tuple-element.44.idx_ref) | copy-start | bytes 73732
  30.4 2.2 copy-start
  37.1 42.7 %copy-start.30 = (s32[1,2,128]{2,1,0:T(2,128)S(1)}, s32[1,2,128]{2,1,0:T(2,128)}, u32[]{:S(2)}) copy-start(s32[1,2,128]{2,1,0:T(2,128)} %param.17) | copy-start | bytes 3076
  37.1 43.5 %copy-start.29 = (s32[1,2,2,1,128]{4,3,2,1,0:T(1,128)S(1)}, s32[1,2,2,1,128]{4,3,2,1,0:T(1,128)}, u32[]{:S(2)}) copy-start(s32[1,2,2,1,128]{4,3,2,1,0:T(1,128)} %param.15) | copy-start | bytes 6148
  37.1 49.7 %all-to-all-start.1 = ((bf16[64,48,128]{2,1,0:T(8,128)(2,1)}), bf16[64,48,128]{2,1,0:T(8,128)(2,1)S(1)}, u32[]{:S(2)}, u32[]{:S(2)}) async-start(bf16[64,48,128]{2,1,0:T(8,128)(2,1)} %bitcast.15), calls=%async_computation.1 | async-start | bytes 1572864 | tf_op jit(solution)/shard_map/all_to_all | solution.py:490
  41.9 24.2 %collective-permute-start.5 = (bf16[32,1024]{1,0:T(8,128)(2,1)S(1)}, bf16[32,1024]{1,0:T(8,128)(2,1)S(1)}, u32[]{:S(2)}, u32[]{:S(2)}) collective-permute-start(bf16[32,1024]{1,0:T(8,128)(2,1)S(1)} %pad_maximum_fusion.1), channel_id=1, source_target_pairs={{0,8},{1,9},{2,10},{3,11},{4,12},{5,13},{6,14},{7,15},{8,0},{9,1},... | collective-permute-start | bytes 196616 | tf_op jit(solution)/shard_map/ppermute | solution.py:502
  66.1 4.0 %collective-permute-start.6 = (bf16[64,1024]{1,0:T(8,128)(2,1)S(1)}, bf16[64,1024]{1,0:T(8,128)(2,1)S(1)}, u32[]{:S(2)}, u32[]{:S(2)}) collective-permute-start(bf16[64,1024]{1,0:T(8,128)(2,1)S(1)} %pad_maximum_fusion), channel_id=1, source_target_pairs={{0,16},{1,17},{2,18},{3,19},{4,20},{5,21},{6,22},{7,23},{8,24},{9,... | collective-permute-start | bytes 393224 | tf_op jit(solution)/shard_map/ppermute | solution.py:502
  67.5 8.3 %collective-permute-start.7 = (bf16[64,1024]{1,0:T(8,128)(2,1)S(1)}, bf16[64,1024]{1,0:T(8,128)(2,1)S(1)}, u32[]{:S(2)}, u32[]{:S(2)}) collective-permute-start(bf16[64,1024]{1,0:T(8,128)(2,1)S(1)} %pad_maximum_fusion), channel_id=1, source_target_pairs={{0,32},{1,33},{2,34},{3,35},{4,36},{5,37},{6,38},{7,39},{8,40},{9,... | collective-permute-start | bytes 393224 | tf_op jit(solution)/shard_map/ppermute | solution.py:502
  70.1 8.3 %collective-permute-start.8 = (bf16[64,1024]{1,0:T(8,128)(2,1)S(1)}, bf16[64,1024]{1,0:T(8,128)(2,1)S(1)}, u32[]{:S(2)}, u32[]{:S(2)}) collective-permute-start(bf16[64,1024]{1,0:T(8,128)(2,1)S(1)} %pad_maximum_fusion), channel_id=1, source_target_pairs={{0,48},{1,49},{2,50},{3,51},{4,52},{5,53},{6,54},{7,55},{8,56},{9,... | collective-permute-start | bytes 393224 | tf_op jit(solution)/shard_map/ppermute | solution.py:502
  78.4 8.4 %collective-permute-start.9 = (bf16[256,1024]{1,0:T(8,128)(2,1)S(1)}, bf16[256,1024]{1,0:T(8,128)(2,1)S(1)}, u32[]{:S(2)}, u32[]{:S(2)}) collective-permute-start(bf16[256,1024]{1,0:T(8,128)(2,1)S(1)} %constant_dynamic-update-slice_fusion.wa_ref), channel_id=1, source_target_pairs={{0,1},{1,0},{2,3},{3,2},{4,5},{5,4},{6,7},{7,6},{8,9},{9,8},{10,11... | collective-permute-start | bytes 1572872 | tf_op jit(solution)/shard_map/ppermute | solution.py:502
  94.2 2.0 collective-permute-start.10
  96.4 5.0 %collective-permute-start.11 = (bf16[64,1024]{1,0:T(8,128)(2,1)S(1)}, bf16[64,1024]{1,0:T(8,128)(2,1)S(1)}, u32[]{:S(2)}, u32[]{:S(2)}) collective-permute-start(bf16[64,1024]{1,0:T(8,128)(2,1)S(1)} %get-tuple-element.73), channel_id=1, source_target_pairs={{0,16},{1,17},{2,18},{3,19},{4,20},{5,21},{6,22},{7,23},{8,24},{9,... | collective-permute-start | bytes 393224 | tf_op jit(solution)/shard_map/ppermute | solution.py:502
  96.5 7.6 %collective-permute-start.12 = (bf16[64,1024]{1,0:T(8,128)(2,1)S(1)}, bf16[64,1024]{1,0:T(8,128)(2,1)S(1)}, u32[]{:S(2)}, u32[]{:S(2)}) collective-permute-start(bf16[64,1024]{1,0:T(8,128)(2,1)S(1)} %get-tuple-element.75), channel_id=1, source_target_pairs={{0,32},{1,33},{2,34},{3,35},{4,36},{5,37},{6,38},{7,39},{8,40},{9,... | collective-permute-start | bytes 393224 | tf_op jit(solution)/shard_map/ppermute | solution.py:502
  97.8 8.8 %collective-permute-start.13 = (bf16[64,1024]{1,0:T(8,128)(2,1)S(1)}, bf16[64,1024]{1,0:T(8,128)(2,1)S(1)}, u32[]{:S(2)}, u32[]{:S(2)}) collective-permute-start(bf16[64,1024]{1,0:T(8,128)(2,1)S(1)} %get-tuple-element.74), channel_id=1, source_target_pairs={{0,48},{1,49},{2,50},{3,51},{4,52},{5,53},{6,54},{7,55},{8,56},{9,... | collective-permute-start | bytes 393224 | tf_op jit(solution)/shard_map/ppermute | solution.py:502
  106.7 20.2 %copy-start.24 = (f32[6,1024]{1,0:T(8,128)S(1)}, f32[6,1024]{1,0:T(8,128)}, u32[]{:S(2)}) copy-start(f32[6,1024]{1,0:T(8,128)} %param.19) | copy-start | bytes 73732
  106.7 43.0 %copy-start.7 = (s32[48,128]{1,0:T(8,128)S(1)}, s32[48,128]{1,0:T(8,128)}, u32[]{:S(2)}) copy-start(s32[48,128]{1,0:T(8,128)} %copy-done.6) | copy-start | bytes 73732
  106.7 43.0 %copy-start.21 = (s32[1,128]{1,0:T(1,128)S(1)}, s32[1,128]{1,0:T(1,128)}, u32[]{:S(2)}) copy-start(s32[1,128]{1,0:T(1,128)} %copy-done.20) | copy-start | bytes 1540
  106.8 7.2 %collective-permute-start.14 = (bf16[32,1024]{1,0:T(8,128)(2,1)S(1)}, bf16[32,1024]{1,0:T(8,128)(2,1)S(1)}, u32[]{:S(2)}, u32[]{:S(2)}) collective-permute-start(bf16[32,1024]{1,0:T(8,128)(2,1)S(1)} %slice.352), channel_id=1, source_target_pairs={{0,8},{1,9},{2,10},{3,11},{4,12},{5,13},{6,14},{7,15},{8,0},{9,1},... | collective-permute-start | bytes 196616 | tf_op jit(solution)/shard_map/ppermute | solution.py:502
  114.0 12.8 %collective-permute-start.15 = (f32[8,1024]{1,0:T(8,128)S(1)}, f32[8,1024]{1,0:T(8,128)S(1)}, u32[]{:S(2)}, u32[]{:S(2)}) collective-permute-start(f32[8,1024]{1,0:T(8,128)S(1)} %get-tuple-element.79), channel_id=1, source_target_pairs={{0,2},{1,3},{2,0},{3,1},{4,6},{5,7},{6,4},{7,5},{8,10},{9,11},{10,... | collective-permute-start | bytes 98312 | tf_op jit(solution)/shard_map/ppermute | solution.py:502
  116.1 10.7 %collective-permute-start.16 = (f32[8,1024]{1,0:T(8,128)S(1)}, f32[8,1024]{1,0:T(8,128)S(1)}, u32[]{:S(2)}, u32[]{:S(2)}) collective-permute-start(f32[8,1024]{1,0:T(8,128)S(1)} %get-tuple-element.81), channel_id=1, source_target_pairs={{0,4},{1,5},{2,6},{3,7},{4,0},{5,1},{6,2},{7,3},{8,12},{9,13},{10,... | collective-permute-start | bytes 98312 | tf_op jit(solution)/shard_map/ppermute | solution.py:502
  116.1 10.7 %collective-permute-start.17 = (f32[8,1024]{1,0:T(8,128)S(1)}, f32[8,1024]{1,0:T(8,128)S(1)}, u32[]{:S(2)}, u32[]{:S(2)}) collective-permute-start(f32[8,1024]{1,0:T(8,128)S(1)} %get-tuple-element.80), channel_id=1, source_target_pairs={{0,6},{1,7},{2,4},{3,5},{4,2},{5,3},{6,0},{7,1},{8,14},{9,15},{10,... | collective-permute-start | bytes 98312 | tf_op jit(solution)/shard_map/ppermute | solution.py:502
  118.4 31.2 %all-to-all-start.2 = ((bf16[64,48,128]{2,1,0:T(8,128)(2,1)}), bf16[64,48,128]{2,1,0:T(8,128)(2,1)S(1)}, u32[]{:S(2)}, u32[]{:S(2)}) async-start(bf16[64,48,128]{2,1,0:T(8,128)(2,1)} %bitcast.17), calls=%async_computation.2 | async-start | bytes 1572864 | tf_op jit(solution)/shard_map/all_to_all | solution.py:490
  159.1 40.4 %copy-start.27 = (f32[1,1,128,13]{2,1,3,0:T(1,128)S(1)}, f32[1,1,128,13]{2,1,3,0:T(1,128)}, u32[]{:S(2)}) copy-start(f32[1,1,128,13]{2,1,3,0:T(1,128)} %get-tuple-element.87) | copy-start | bytes 19972
  159.1 40.5 %copy-start.28 = (f32[128,1]{0,1:T(1,128)S(1)}, f32[128,1]{0,1:T(1,128)}, u32[]{:S(2)}) copy-start(f32[128,1]{0,1:T(1,128)} %get-tuple-element.97) | copy-start | bytes 1540
  159.1 40.6 %copy-start.17 = (s32[2,512]{1,0:T(2,128)S(1)}, s32[2,512]{1,0:T(2,128)}, u32[]{:S(2)}) copy-start(s32[2,512]{1,0:T(2,128)} %get-tuple-element.89.slot_ref) | copy-start | bytes 12292
  159.1 40.6 %copy-start.19 = (s32[2,128]{1,0:T(2,128)S(1)}, s32[2,128]{1,0:T(2,128)}, u32[]{:S(2)}) copy-start(s32[2,128]{1,0:T(2,128)} %get-tuple-element.95.bag_ref) | copy-start | bytes 3076
  159.2 44.6 %copy-start.16 = (s32[2]{0:T(128)S(1)}, s32[2]{0:T(128)}, u32[]{:S(2)}) copy-start(s32[2]{0:T(128)} %copy-done.14) | copy-start | bytes 28
  199.4 4.3 %collective-permute-start.18 = (bf16[64,32,128]{2,1,0:T(8,128)(2,1)S(1)}, bf16[64,32,128]{2,1,0:T(8,128)(2,1)S(1)}, u32[]{:S(2)}, u32[]{:S(2)}) collective-permute-start(bf16[64,32,128]{2,1,0:T(8,128)(2,1)S(1)} %slice.279), channel_id=1, source_target_pairs={{0,1},{1,0},{2,3},{3,2},{4,5},{5,4},{6,7},{7,6},{8,9},{9,8},{10,11... | collective-permute-start | bytes 1572872 | tf_op jit(solution)/shard_map/ppermute | solution.py:502
  210.6 6.9 %collective-permute-start.28 = (bf16[256,1024]{1,0:T(8,128)(2,1)S(1)}, bf16[256,1024]{1,0:T(8,128)(2,1)}, u32[]{:S(2)}, u32[]{:S(2)}) collective-permute-start(bf16[256,1024]{1,0:T(8,128)(2,1)S(1)} %get-tuple-element.59), channel_id=1, source_target_pairs={{0,1},{1,0},{2,3},{3,2},{4,5},{5,4},{6,7},{7,6},{8,9},{9,8},{10,11... | collective-permute-start | bytes 1572872 | tf_op jit(solution)/shard_map/ppermute | solution.py:502
  211.2 48.2 %all-to-all-start.4 = ((bf16[64,48,128]{2,1,0:T(8,128)(2,1)}), bf16[64,48,128]{2,1,0:T(8,128)(2,1)}, u32[]{:S(2)}, u32[]{:S(2)}) async-start(bf16[64,48,128]{2,1,0:T(8,128)(2,1)} %bitcast.21), calls=%async_computation.4 | async-start | bytes 1572864 | tf_op jit(solution)/shard_map/all_to_all | solution.py:490
  217.5 5.6 %copy-start.31 = (s32[16]{0:T(128)S(1)}, s32[16]{0:T(128)}, u32[]{:S(2)}) copy-start(s32[16]{0:T(128)} %param.21) | copy-start | bytes 196
  218.8 24.1 %copy-start.23 = (s32[64,1,96]{2,1,0:T(1,128)S(1)}, s32[64,1,96]{2,1,0:T(1,128)}, u32[]{:S(2)}) copy-start(s32[64,1,96]{2,1,0:T(1,128)} %copy-done.22) | copy-start | bytes 73732
  218.9 6.8 %collective-permute-start.29 = (bf16[64,1024]{1,0:T(8,128)(2,1)S(1)}, bf16[64,1024]{1,0:T(8,128)(2,1)S(1)}, u32[]{:S(2)}, u32[]{:S(2)}) collective-permute-start(bf16[64,1024]{1,0:T(8,128)(2,1)S(1)} %get-tuple-element.70), channel_id=1, source_target_pairs={{0,16},{1,17},{2,18},{3,19},{4,20},{5,21},{6,22},{7,23},{8,24},{9,... | collective-permute-start | bytes 393224 | tf_op jit(solution)/shard_map/ppermute | solution.py:502
  220.5 13.4 %collective-permute-start.30 = (bf16[64,1024]{1,0:T(8,128)(2,1)S(1)}, bf16[64,1024]{1,0:T(8,128)(2,1)S(1)}, u32[]{:S(2)}, u32[]{:S(2)}) collective-permute-start(bf16[64,1024]{1,0:T(8,128)(2,1)S(1)} %get-tuple-element.72), channel_id=1, source_target_pairs={{0,32},{1,33},{2,34},{3,35},{4,36},{5,37},{6,38},{7,39},{8,40},{9,... | collective-permute-start | bytes 393224 | tf_op jit(solution)/shard_map/ppermute | solution.py:502
  223.1 13.8 %collective-permute-start.31 = (bf16[64,1024]{1,0:T(8,128)(2,1)S(1)}, bf16[64,1024]{1,0:T(8,128)(2,1)S(1)}, u32[]{:S(2)}, u32[]{:S(2)}) collective-permute-start(bf16[64,1024]{1,0:T(8,128)(2,1)S(1)} %get-tuple-element.71), channel_id=1, source_target_pairs={{0,48},{1,49},{2,50},{3,51},{4,52},{5,53},{6,54},{7,55},{8,56},{9,... | collective-permute-start | bytes 393224 | tf_op jit(solution)/shard_map/ppermute | solution.py:502
  236.9 10.9 %collective-permute-start.32 = (bf16[32,1024]{1,0:T(8,128)(2,1)S(1)}, bf16[32,1024]{1,0:T(8,128)(2,1)S(1)}, u32[]{:S(2)}, u32[]{:S(2)}) collective-permute-start(bf16[32,1024]{1,0:T(8,128)(2,1)S(1)} %slice.351), channel_id=1, source_target_pairs={{0,8},{1,9},{2,10},{3,11},{4,12},{5,13},{6,14},{7,15},{8,0},{9,1},... | collective-permute-start | bytes 196616 | tf_op jit(solution)/shard_map/ppermute | solution.py:502
  242.9 6.7 %collective-permute-start = (s32[64,96]{1,0:T(8,128)S(1)}, s32[64,96]{1,0:T(8,128)S(1)}, u32[]{:S(2)}, u32[]{:S(2)}) collective-permute-start(s32[64,96]{1,0:T(8,128)S(1)} %bitcast.56), channel_id=1, source_target_pairs={{0,64},{64,128},{128,192},{192,0},{1,65},{65,129},{129,193},{193,1... | collective-permute-start | bytes 73736 | tf_op jit(solution)/shard_map/ppermute | solution.py:494
  244.2 7.3 %collective-permute-start.1 = (s32[64,96]{1,0:T(8,128)S(1)}, s32[64,96]{1,0:T(8,128)S(1)}, u32[]{:S(2)}, u32[]{:S(2)}) collective-permute-start(s32[64,96]{1,0:T(8,128)S(1)} %bitcast.57), channel_id=1, source_target_pairs={{0,128},{64,192},{128,0},{192,64},{1,129},{65,193},{129,1},{193,65... | collective-permute-start | bytes 73736 | tf_op jit(solution)/shard_map/ppermute | solution.py:494
  246.7 4.8 %collective-permute-start.2 = (s32[64,96]{1,0:T(8,128)S(1)}, s32[64,96]{1,0:T(8,128)S(1)}, u32[]{:S(2)}, u32[]{:S(2)}) collective-permute-start(s32[64,96]{1,0:T(8,128)S(1)} %bitcast.58), channel_id=1, source_target_pairs={{0,192},{64,0},{128,64},{192,128},{1,193},{65,1},{129,65},{193,129... | collective-permute-start | bytes 73736 | tf_op jit(solution)/shard_map/ppermute | solution.py:494
  247.9 7.7 %collective-permute-start.33 = (f32[8,1024]{1,0:T(8,128)S(1)}, f32[8,1024]{1,0:T(8,128)S(1)}, u32[]{:S(2)}, u32[]{:S(2)}) collective-permute-start(f32[8,1024]{1,0:T(8,128)S(1)} %get-tuple-element.76), channel_id=1, source_target_pairs={{0,2},{1,3},{2,0},{3,1},{4,6},{5,7},{6,4},{7,5},{8,10},{9,11},{10,... | collective-permute-start | bytes 98312 | tf_op jit(solution)/shard_map/ppermute | solution.py:502
  248.9 7.4 %collective-permute-start.34 = (f32[8,1024]{1,0:T(8,128)S(1)}, f32[8,1024]{1,0:T(8,128)S(1)}, u32[]{:S(2)}, u32[]{:S(2)}) collective-permute-start(f32[8,1024]{1,0:T(8,128)S(1)} %get-tuple-element.78), channel_id=1, source_target_pairs={{0,4},{1,5},{2,6},{3,7},{4,0},{5,1},{6,2},{7,3},{8,12},{9,13},{10,... | collective-permute-start | bytes 98312 | tf_op jit(solution)/shard_map/ppermute | solution.py:502
  249.6 6.7 %collective-permute-start.35 = (f32[8,1024]{1,0:T(8,128)S(1)}, f32[8,1024]{1,0:T(8,128)S(1)}, u32[]{:S(2)}, u32[]{:S(2)}) collective-permute-start(f32[8,1024]{1,0:T(8,128)S(1)} %get-tuple-element.77), channel_id=1, source_target_pairs={{0,6},{1,7},{2,4},{3,5},{4,2},{5,3},{6,0},{7,1},{8,14},{9,15},{10,... | collective-permute-start | bytes 98312 | tf_op jit(solution)/shard_map/ppermute | solution.py:502
  253.6 41.1 %collective-permute-start.25 = (bf16[64,48,128]{2,1,0:T(8,128)(2,1)S(1)}, bf16[64,48,128]{2,1,0:T(8,128)(2,1)S(1)}, u32[]{:S(2)}, u32[]{:S(2)}) collective-permute-start(bf16[64,48,128]{2,1,0:T(8,128)(2,1)S(1)} %all-to-all-done.2.refs_0_), channel_id=1, source_target_pairs={{0,64},{64,128},{128,192},{192,0},{1,65},{65,129},{129,193},{193,1... | collective-permute-start | bytes 2359304 | tf_op jit(solution)/shard_map/ppermute | solution.py:494
  253.9 42.7 %collective-permute-start.26 = (bf16[64,48,128]{2,1,0:T(8,128)(2,1)S(1)}, bf16[64,48,128]{2,1,0:T(8,128)(2,1)S(1)}, u32[]{:S(2)}, u32[]{:S(2)}) collective-permute-start(bf16[64,48,128]{2,1,0:T(8,128)(2,1)S(1)} %all-to-all-done.2.refs_0_), channel_id=1, source_target_pairs={{0,128},{64,192},{128,0},{192,64},{1,129},{65,193},{129,1},{193,65... | collective-permute-start | bytes 2359304 | tf_op jit(solution)/shard_map/ppermute | solution.py:494
  255.6 41.7 %collective-permute-start.27 = (bf16[64,48,128]{2,1,0:T(8,128)(2,1)S(1)}, bf16[64,48,128]{2,1,0:T(8,128)(2,1)S(1)}, u32[]{:S(2)}, u32[]{:S(2)}) collective-permute-start(bf16[64,48,128]{2,1,0:T(8,128)(2,1)S(1)} %all-to-all-done.2.refs_0_), channel_id=1, source_target_pairs={{0,192},{64,0},{128,64},{192,128},{1,193},{65,1},{129,65},{193,129... | collective-permute-start | bytes 2359304 | tf_op jit(solution)/shard_map/ppermute | solution.py:494
  257.0 31.3 %collective-permute-start.36 = (f32[8,1024]{1,0:T(8,128)}, f32[8,1024]{1,0:T(8,128)}, u32[]{:S(2)}, u32[]{:S(2)}) collective-permute-start(f32[8,1024]{1,0:T(8,128)} %fusion.7), channel_id=1, source_target_pairs={{0,128},{64,192},{128,0},{192,64},{1,129},{65,193},{129,1},{193,65... | collective-permute-start | bytes 98312 | tf_op jit(solution)/shard_map/ppermute | solution.py:494
  259.3 31.8 %collective-permute-start.37 = (f32[8,1024]{1,0:T(8,128)}, f32[8,1024]{1,0:T(8,128)}, u32[]{:S(2)}, u32[]{:S(2)}) collective-permute-start(f32[8,1024]{1,0:T(8,128)} %fusion.7), channel_id=1, source_target_pairs={{0,64},{64,128},{128,192},{192,0},{1,65},{65,129},{129,193},{193,1... | collective-permute-start | bytes 98312 | tf_op jit(solution)/shard_map/ppermute | solution.py:494
  259.3 31.8 %copy-start.11 = (s32[4,2,24,128]{3,2,1,0:T(8,128)S(1)}, s32[4,2,24,128]{3,2,1,0:T(8,128)}, u32[]{:S(2)}) copy-start(s32[4,2,24,128]{3,2,1,0:T(8,128)} %copy-done.10) | copy-start | bytes 294916
  288.3 4.2 %collective-permute-start.38 = (f32[8,1024]{1,0:T(8,128)}, f32[8,1024]{1,0:T(8,128)S(1)}, u32[]{:S(2)}, u32[]{:S(2)}) collective-permute-start(f32[8,1024]{1,0:T(8,128)} %fusion.7), channel_id=1, source_target_pairs={{0,192},{64,0},{128,64},{192,128},{1,193},{65,1},{129,65},{193,129... | collective-permute-start | bytes 98312 | tf_op jit(solution)/shard_map/ppermute | solution.py:494
  291.1 11.9 %collective-permute-start.22 = (bf16[64,24,128]{2,1,0:T(8,128)(2,1)}, bf16[64,24,128]{2,1,0:T(8,128)(2,1)S(1)}, u32[]{:S(2)}, u32[]{:S(2)}) collective-permute-start(bf16[64,24,128]{2,1,0:T(8,128)(2,1)} %get-tuple-element.68.refs_0_), channel_id=1, source_target_pairs={{0,64},{64,128},{128,192},{192,0},{1,65},{65,129},{129,193},{193,1... | collective-permute-start | bytes 1179656 | tf_op jit(solution)/shard_map/ppermute | solution.py:494
  293.3 10.6 %copy-start.26 = (f32[8,1024]{1,0:T(8,128)}, f32[8,1024]{1,0:T(8,128)S(1)}, u32[]{:S(2)}) copy-start(f32[8,1024]{1,0:T(8,128)S(1)} %add_add_fusion) | copy-start | bytes 98308
  293.3 62.9 %collective-permute-start.23 = (bf16[64,24,128]{2,1,0:T(8,128)(2,1)}, bf16[64,24,128]{2,1,0:T(8,128)(2,1)}, u32[]{:S(2)}, u32[]{:S(2)}) collective-permute-start(bf16[64,24,128]{2,1,0:T(8,128)(2,1)} %get-tuple-element.68.refs_0_), channel_id=1, source_target_pairs={{0,128},{64,192},{128,0},{192,64},{1,129},{65,193},{129,1},{193,65... | collective-permute-start | bytes 1179656 | tf_op jit(solution)/shard_map/ppermute | solution.py:494
  294.7 61.5 %collective-permute-start.24 = (bf16[64,24,128]{2,1,0:T(8,128)(2,1)}, bf16[64,24,128]{2,1,0:T(8,128)(2,1)}, u32[]{:S(2)}, u32[]{:S(2)}) collective-permute-start(bf16[64,24,128]{2,1,0:T(8,128)(2,1)} %get-tuple-element.68.refs_0_), channel_id=1, source_target_pairs={{0,192},{64,0},{128,64},{192,128},{1,193},{65,1},{129,65},{193,129... | collective-permute-start | bytes 1179656 | tf_op jit(solution)/shard_map/ppermute | solution.py:494
  296.7 77.2 %collective-permute-start.19 = (bf16[64,24,128]{2,1,0:T(8,128)(2,1)S(1)}, bf16[64,24,128]{2,1,0:T(8,128)(2,1)}, u32[]{:S(2)}, u32[]{:S(2)}) collective-permute-start(bf16[64,24,128]{2,1,0:T(8,128)(2,1)S(1)} %get-tuple-element.69.refs_0_), channel_id=1, source_target_pairs={{0,64},{64,128},{128,192},{192,0},{1,65},{65,129},{129,193},{193,1... | collective-permute-start | bytes 1179656 | tf_op jit(solution)/shard_map/ppermute | solution.py:494
  297.2 76.6 %collective-permute-start.20 = (bf16[64,24,128]{2,1,0:T(8,128)(2,1)S(1)}, bf16[64,24,128]{2,1,0:T(8,128)(2,1)}, u32[]{:S(2)}, u32[]{:S(2)}) collective-permute-start(bf16[64,24,128]{2,1,0:T(8,128)(2,1)S(1)} %get-tuple-element.69.refs_0_), channel_id=1, source_target_pairs={{0,128},{64,192},{128,0},{192,64},{1,129},{65,193},{129,1},{193,65... | collective-permute-start | bytes 1179656 | tf_op jit(solution)/shard_map/ppermute | solution.py:494
  303.8 70.0 %collective-permute-start.21 = (bf16[64,24,128]{2,1,0:T(8,128)(2,1)S(1)}, bf16[64,24,128]{2,1,0:T(8,128)(2,1)}, u32[]{:S(2)}, u32[]{:S(2)}) collective-permute-start(bf16[64,24,128]{2,1,0:T(8,128)(2,1)S(1)} %get-tuple-element.69.refs_0_), channel_id=1, source_target_pairs={{0,192},{64,0},{128,64},{192,128},{1,193},{65,1},{129,65},{193,129... | collective-permute-start | bytes 1179656 | tf_op jit(solution)/shard_map/ppermute | solution.py:494
  304.5 49.2 %all-to-all-start.5 = ((f32[64,1,128]{2,1,0:T(1,128)}), f32[64,1,128]{2,1,0:T(1,128)}, u32[]{:S(2)}, u32[]{:S(2)}) async-start(f32[64,1,128]{2,1,0:T(1,128)} %broadcast_in_dim.34), calls=%async_computation.5 | async-start | bytes 65536 | tf_op jit(solution)/shard_map/all_to_all | solution.py:490
  325.5 14.2 %copy-start.13 = (s32[2,24,128]{2,1,0:T(8,128)S(1)}, s32[2,24,128]{2,1,0:T(8,128)}, u32[]{:S(2)}) copy-start(s32[2,24,128]{2,1,0:T(8,128)} %get-tuple-element.83.idx_ref) | copy-start | bytes 73732
  358.0 15.9 %copy-start.8 = (s32[2,24,128]{2,1,0:T(8,128)S(1)}, s32[2,24,128]{2,1,0:T(8,128)}, u32[]{:S(2)}) copy-start(s32[2,24,128]{2,1,0:T(8,128)} %get-tuple-element.85.idx_ref) | copy-start | bytes 73732
  (12 other events, 10.9 us)

commit v2 on v1

--- a/solution.py
+++ b/solution.py
@@ -280,35 +280,56 @@
     def total_kernel(me_ref, weight_ref, idx_ref, clash_ref, *refs):
         lists = refs[:NG]
         old, out_ref = (refs[NG], refs[NG + 1]) if step or t else (None, refs[NG])
-        acc0, acc1, part, stage0, stage1, sems, acc_sem = refs[-7:]
+        acc0, acc1, part, stage0, stage1, sems, acc_sem, out_sems = refs[-8:]
         group = me_ref[1]
-        apart = [(group + NG - k) % NG for k in range(NG)]
 
         def list_copy(d, k):
             rows = lists[d].at[:, pl.ds(0 if step else t * CAP, CAP), :]
             return pltpu.make_async_copy(rows, part.at[k], sems.at[k])
 
-        for k in range(NG):
+        def apart(k):
+            return (group + NG - k) % NG
+
+        def fetch(k, _):
             for d in range(NG):
 
-                @pl.when(apart[k] == d)
-                def _(d=d, k=k):
+                @pl.when(apart(k) == d)
+                def _(d=d):
                     list_copy(d, k).start()
 
+            return 0
+
+        lax.fori_loop(0, NG, fetch, 0)
         if step:
             seed = pltpu.make_async_copy(old.at[t], acc0, acc_sem)
             seed.start()
-        else:
-            acc0[...] = jnp.zeros(acc0.shape, f32)
-        acc1[...] = jnp.zeros(acc1.shape, f32)
-        for k in range(0, NG, 2):
-            for i, stage in enumerate((stage0, stage1)):
-                list_copy(0, k + i).wait()
-                stage[...] = part[k + i].reshape(NS * CAP, EMB).astype(f32) * weight_ref[k + i]
-            if step and k == 0:
-                seed.wait()
-            halves = [apart[k + i] // 2 for i in range(2)]
-            sources = [(apart[k + i] % 2) * NS for i in range(2)]
+
+        def clear(c, _):
+            rows = pl.ds(pl.multiple_of(c * 512, 512), 512)
+            zero = jnp.zeros((512, EMB), f32)
+            if not step:
+                acc0[rows, :] = zero
+            acc1[rows, :] = zero
+            return 0
+
+        lax.fori_loop(0, ROWS // 512, clear, 0)
+        if step:
+            seed.wait()
+
+        def pair(p, _):
+            ks = [2 * p, 2 * p + 1]
+            for k, stage in zip(ks, (stage0, stage1)):
+                list_copy(0, k).wait()
+
+                def widen(c, _):
+                    rows = part[k, pl.ds(c * 16, 16)].reshape(16 * CAP, EMB)
+                    at = pl.multiple_of(c * 16 * CAP, 16 * CAP)
+                    stage[pl.ds(at, 16 * CAP), :] = rows.astype(f32) * weight_ref[k]
+                    return 0
+
+                lax.fori_loop(0, NS // 16, widen, 0)
+            halves = [apart(k) // 2 for k in ks]
+            sources = [(apart(k) % 2) * NS for k in ks]
             add_rows(
                 [
                     (
@@ -324,10 +345,27 @@
                 + clash_ref.at[halves[1]][sources[1] + s]
                 == 0,
             )
-        acc0[...] = acc0[...] + acc1[...]
-        result = pltpu.make_async_copy(acc0, out_ref.at[t], acc_sem)
-        result.start()
-        result.wait()
+            return 0
+
+        lax.fori_loop(0, NG // 2, pair, 0)
+
+        def result(c):
+            rows = pl.ds(pl.multiple_of(c * 1024, 1024), 1024)
+            return pltpu.make_async_copy(acc0.at[rows], out_ref.at[t, rows], out_sems.at[c])
+
+        def finish(c, _):
+            for half in range(2):
+                rows = pl.ds(pl.multiple_of(c * 1024 + half * 512, 512), 512)
+                acc0[rows, :] = acc0[rows, :] + acc1[rows, :]
+            result(c).start()
+            return 0
+
+        def drain(c, _):
+            result(c).wait()
+            return 0
+
+        lax.fori_loop(0, ROWS // 1024, finish, 0)
+        lax.fori_loop(0, ROWS // 1024, drain, 0)
 
     return total_kernel
 
@@ -349,6 +387,7 @@
             pltpu.VMEM((NS * CAP, EMB), f32),
             pltpu.SemaphoreType.DMA((NG,)),
             pltpu.SemaphoreType.DMA,
+            pltpu.SemaphoreType.DMA((ROWS // 1024,)),
         ],
         compiler_params=params(16),
     )(*operands)

time: 397 us -> 397 us (level)
  no operation moved by 1% of the time
where the time goes in v2:
time: 397 us; the launch traced here: 390 us
  waiting for transfers between devices  114 us (29%)
  starting transfers between devices  107 us (27%)
  Pallas kernels  95.2 us (24%)
  blocking collectives  40.2 us (10%)
  local copies, waits for them, and re-layouts  25.3 us (6%)
  other arithmetic  6.07 us (2%)
    pallas_call x4, Pallas kernels, add_lists(): pl.pallas_call(make_total_kernel(step, t), in_specs=[sm, sm, sm, sm] + [h...  59.8 us
    ppermute x24, waiting for transfers between devices, swap(): return lax.ppermute(x, 'shard', [(i, i ^ bits) for i in range(NS)])  56 us
    all_to_all x5, starting transfers between devices, exchange(): return lax.all_to_all(x, 'shard', 0, 0, tiled=True)  50.8 us
    all_to_all x1, blocking collectives, exchange(): return lax.all_to_all(x, 'shard', 0, 0, tiled=True)  40.2 us
    ppermute x24, starting transfers between devices, swap(): return lax.ppermute(x, 'shard', [(i, i ^ bits) for i in range(NS)])  37.4 us
    ppermute x15, waiting for transfers between devices, to_group(): return lax.ppermute(x, 'group', [(i, (i + d) % NG) for i in range(NG)])  31.8 us
    all_to_all x5, waiting for transfers between devices, exchange(): return lax.all_to_all(x, 'shard', 0, 0, tiled=True)  26.6 us
    ppermute x15, starting transfers between devices, to_group(): return lax.ppermute(x, 'group', [(i, (i + d) % NG) for i in range(NG)])  18.5 us
  transfers between devices with their start and end apart: 44, of which 16 were waited for; matrix products, arithmetic and copies ran while one was open for 4% of the time, Pallas kernels for 15%

profile of v2, /device:TPU:1, one launch (start us, length us, event | category | flops | bytes accessed | tf_op | source)
XLA Modules:
  0.0 389.9 jit_solution(7538400628156804770)
XLA Ops:
  1.4 2.5 collective-permute-start.3
  5.4 2.5 route.1
  8.4 11.7 %all-to-all-start = ((s32[64,1,96]{2,1,0:T(1,128)}), s32[64,1,96]{2,1,0:T(1,128)S(1)}, u32[]{:S(2)}, u32[]{:S(2)}) async-start(s32[64,1,96]{2,1,0:T(1,128)} %bitcast.3), calls=%async_computation | async-start | bytes 65536 | tf_op jit(solution)/shard_map/all_to_all | solution.py:529
  21.0 2.3 collective-permute-start.4
  23.4 1.4 fusion.21
  24.8 4.7 %all-to-all-done = s32[64,1,96]{2,1,0:T(1,128)S(1)} async-done(((s32[64,1,96]{2,1,0:T(1,128)}), s32[64,1,96]{2,1,0:T(1,128)S(1)}, u32[]{:S(2)}, u32[]{:S(2)}) %all-to-all-start) | async-done | bytes 24608 | tf_op jit(solution)/shard_map/all_to_all | solution.py:529
  30.5 2.2 copy-done
  32.6 4.4 %gather_first.1 = bf16[3072,128]{1,0:T(8,128)(2,1)} custom-call(s32[48,128]{1,0:T(8,128)S(1)} %get-tuple-element.44.idx_ref, bf16[2,8192,128]{2,1,0:T(8,128)(2,1)S(1)} %copy-done), custom_call_target="tpu_custom_call" | custom-call | tf_op jit(solution)/shard_map/gather_first/pallas_call | solution.py:227
  37.1 4.8 %all-to-all-start.1 = ((bf16[64,48,128]{2,1,0:T(8,128)(2,1)}), bf16[64,48,128]{2,1,0:T(8,128)(2,1)S(1)}, u32[]{:S(2)}, u32[]{:S(2)}) async-start(bf16[64,48,128]{2,1,0:T(8,128)(2,1)} %bitcast.15), calls=%async_computation.1 | async-start | bytes 1572864 | tf_op jit(solution)/shard_map/all_to_all | solution.py:529
  41.9 5.4 %collective-permute-start.5 = (bf16[32,1024]{1,0:T(8,128)(2,1)S(1)}, bf16[32,1024]{1,0:T(8,128)(2,1)S(1)}, u32[]{:S(2)}, u32[]{:S(2)}) collective-permute-start(bf16[32,1024]{1,0:T(8,128)(2,1)S(1)} %pad_maximum_fusion.1), channel_id=1, source_target_pairs={{0,8},{1,9},{2,10},{3,11},{4,12},{5,13},{6,14},{7,15},{8,0},{9,1},... | collective-permute-start | bytes 196616 | tf_op jit(solution)/shard_map/ppermute | solution.py:541
  47.3 18.8 %collective-permute-done.5 = bf16[32,1024]{1,0:T(8,128)(2,1)S(1)} collective-permute-done((bf16[32,1024]{1,0:T(8,128)(2,1)S(1)}, bf16[32,1024]{1,0:T(8,128)(2,1)S(1)}, u32[]{:S(2)}, u32[]{:S(2)}) %collective-permute-start.5) | collective-permute-done | bytes 65568 | tf_op jit(solution)/shard_map/ppermute | solution.py:541
  66.1 1.4 collective-permute-start.6
  67.5 2.6 collective-permute-start.7
  70.2 5.6 %collective-permute-done.7 = bf16[64,1024]{1,0:T(8,128)(2,1)S(1)} collective-permute-done((bf16[64,1024]{1,0:T(8,128)(2,1)S(1)}, bf16[64,1024]{1,0:T(8,128)(2,1)S(1)}, u32[]{:S(2)}, u32[]{:S(2)}) %collective-permute-start.7) | collective-permute-done | bytes 131104 | tf_op jit(solution)/shard_map/ppermute | solution.py:541
  75.8 2.6 collective-permute-done.8
  78.4 1.4 collective-permute-start.9
  81.7 3.9 %pool_matrix.3 = (bf16[256,3072]{1,0:T(8,128)(2,1)S(1)}, bf16[3072,256]{1,0:T(8,128)(2,1)S(1)}) custom-call(s32[2,512]{1,0:T(2,128)S(1)} %get-tuple-element.88.slot_ref, s32[2,128]{1,0:T(2,128)S(1)} %get-tuple-element.94.bag_ref), custom_call_target="tpu_custom_call" | custom-call | tf_op jit(solution)/shard_map/pool_matrix/pallas_call | solution.py:114
  85.7 1.1 copy-done.2
  86.8 1.4 copy-done.3
  88.9 3.9 %shard_map.131 = (bf16[3072,128]{1,0:T(8,128)(2,1)}, bf16[128,384]{1,0:T(8,128)(2,1)S(1)}, bf16[128,1024]{1,0:T(8,128)(2,1)S(1)}, f32[32,128]{1,0:T(8,128)S(1)}) custom-call(s32[2]{0:T(128)S(1)} %copy-done.15, bf16[256,3072]{1,0:T(8,128)(2,1)S(1)} %get-tuple-element.46.a_ref, bf16[3072,256]{1,0:T(8,128)(2,1)S(1)} %copy-done.3, f32[128,13]{1,0:T(8,128)S(1)} %bitcast.52, ...), custom_call_target="tpu_custom_call" | custom-call | tf_op jit(solution)/shard_map/pallas_call | solution.py:488
  92.8 1.4 weight_grad.2
  94.3 1.9 collective-permute-done.10
  96.5 1.3 collective-permute-start.12
  97.8 2.5 collective-permute-start.13
  101.4 2.7 collective-permute-done.12
  104.1 2.5 collective-permute-done.13
  106.9 7.1 %collective-permute-done.14 = bf16[32,1024]{1,0:T(8,128)(2,1)S(1)} collective-permute-done((bf16[32,1024]{1,0:T(8,128)(2,1)S(1)}, bf16[32,1024]{1,0:T(8,128)(2,1)S(1)}, u32[]{:S(2)}, u32[]{:S(2)}) %collective-permute-start.14) | collective-permute-done | bytes 65568 | tf_op jit(solution)/shard_map/ppermute | solution.py:541
  114.0 2.1 collective-permute-start.15
  116.1 2.2 collective-permute-start.17
  118.4 8.4 %all-to-all-start.2 = ((bf16[64,48,128]{2,1,0:T(8,128)(2,1)}), bf16[64,48,128]{2,1,0:T(8,128)(2,1)S(1)}, u32[]{:S(2)}, u32[]{:S(2)}) async-start(bf16[64,48,128]{2,1,0:T(8,128)(2,1)} %bitcast.17), calls=%async_computation.2 | async-start | bytes 1572864 | tf_op jit(solution)/shard_map/all_to_all | solution.py:529
  127.7 21.9 %all-to-all-done.2.refs_0_ = bf16[64,48,128]{2,1,0:T(8,128)(2,1)S(1)} async-done(((bf16[64,48,128]{2,1,0:T(8,128)(2,1)}), bf16[64,48,128]{2,1,0:T(8,128)(2,1)S(1)}, u32[]{:S(2)}, u32[]{:S(2)}) %all-to-all-start.2) | async-done | bytes 786464 | tf_op jit(solution)/shard_map/all_to_all | solution.py:529
  149.6 2.2 copy-done.1
  151.8 7.1 %owner_step.1 = bf16[64,80,128]{2,1,0:T(8,128)(2,1)S(1)} custom-call(s32[48,128]{1,0:T(8,128)S(1)} %copy-done.7, s32[1,128]{1,0:T(1,128)S(1)} %copy-done.21, bf16[3072,128]{1,0:T(8,128)(2,1)S(1)} %bitcast.50, bf16[2,8192,128]{2,1,0:T(8,128)(2,1)S(1)} %copy-done.1), custom_call_target="tpu_custom_call" | custom-call | tf_op jit(solution)/shard_map/owner_step/pallas_call | solution.py:264
  159.2 40.2 %all_to_all.37.wa_ref = bf16[64,80,128]{2,1,0:T(8,128)(2,1)S(1)} all-to-all(bf16[64,80,128]{2,1,0:T(8,128)(2,1)S(1)} %constant_dynamic-update-slice_fusion.15), channel_id=1, replica_groups=mesh['group'=4,'shard'=64] {'shard'}, dimensions={0} | all-to-all | bytes 2621440 | tf_op jit(solution)/shard_map/all_to_all | solution.py:529
  199.7 4.0 %pool_matrix.2 = (bf16[256,3072]{1,0:T(8,128)(2,1)S(1)}, bf16[3072,256]{1,0:T(8,128)(2,1)S(1)}) custom-call(s32[2,512]{1,0:T(2,128)S(1)} %copy-done.17, s32[2,128]{1,0:T(2,128)S(1)} %copy-done.19), custom_call_target="tpu_custom_call" | custom-call | tf_op jit(solution)/shard_map/pool_matrix/pallas_call | solution.py:114
  203.7 5.4 %shard_map.132 = (bf16[3072,128]{1,0:T(8,128)(2,1)}, bf16[128,384]{1,0:T(8,128)(2,1)S(1)}, bf16[128,1024]{1,0:T(8,128)(2,1)S(1)}, f32[32,128]{1,0:T(8,128)S(1)}) custom-call(s32[2]{0:T(128)S(1)} %copy-done.16, bf16[256,3072]{1,0:T(8,128)(2,1)S(1)} %get-tuple-element.42.a_ref, bf16[3072,256]{1,0:T(8,128)(2,1)S(1)} %get-tuple-element.43.at_ref, ...), custom_call_target="tpu_custom_call" | custom-call | tf_op jit(solution)/shard_map/pallas_call | solution.py:488
  209.1 1.4 weight_grad.3
  211.2 6.3 %all-to-all-start.4 = ((bf16[64,48,128]{2,1,0:T(8,128)(2,1)}), bf16[64,48,128]{2,1,0:T(8,128)(2,1)}, u32[]{:S(2)}, u32[]{:S(2)}) async-start(bf16[64,48,128]{2,1,0:T(8,128)(2,1)} %bitcast.21), calls=%async_computation.4 | async-start | bytes 1572864 | tf_op jit(solution)/shard_map/all_to_all | solution.py:529
  217.5 1.3 fusion.13
  218.9 1.6 collective-permute-start.29
  220.5 2.6 collective-permute-start.30
  223.2 2.5 collective-permute-done.29
  225.7 8.2 %collective-permute-done.30 = bf16[64,1024]{1,0:T(8,128)(2,1)S(1)} collective-permute-done((bf16[64,1024]{1,0:T(8,128)(2,1)S(1)}, bf16[64,1024]{1,0:T(8,128)(2,1)S(1)}, u32[]{:S(2)}, u32[]{:S(2)}) %collective-permute-start.30) | collective-permute-done | bytes 131104 | tf_op jit(solution)/shard_map/ppermute | solution.py:541
  233.9 3.0 collective-permute-done.31
  236.9 4.8 %collective-permute-start.32 = (bf16[32,1024]{1,0:T(8,128)(2,1)S(1)}, bf16[32,1024]{1,0:T(8,128)(2,1)S(1)}, u32[]{:S(2)}, u32[]{:S(2)}) collective-permute-start(bf16[32,1024]{1,0:T(8,128)(2,1)S(1)} %slice.351), channel_id=1, source_target_pairs={{0,8},{1,9},{2,10},{3,11},{4,12},{5,13},{6,14},{7,15},{8,0},{9,1},... | collective-permute-start | bytes 196616 | tf_op jit(solution)/shard_map/ppermute | solution.py:541
  242.9 1.3 collective-permute-start
  244.2 2.4 collective-permute-start.1
  246.7 1.2 collective-permute-start.2
  249.6 1.9 collective-permute-start.35
  253.9 1.6 collective-permute-start.26
  257.0 2.3 collective-permute-start.36
  259.3 2.0 fusion.16
  261.3 27.0 %collective-permute-done.36 = f32[8,1024]{1,0:T(8,128)} collective-permute-done((f32[8,1024]{1,0:T(8,128)}, f32[8,1024]{1,0:T(8,128)}, u32[]{:S(2)}, u32[]{:S(2)}) %collective-permute-start.36) | collective-permute-done | bytes 32800 | tf_op jit(solution)/shard_map/ppermute | solution.py:533
  288.3 2.9 collective-permute-start.38
  293.3 1.4 collective-permute-start.23
  294.7 1.9 collective-permute-start.24
  297.2 1.8 collective-permute-start.20
  299.0 4.1 %collective-permute-done.22.refs_1_ = bf16[64,24,128]{2,1,0:T(8,128)(2,1)S(1)} collective-permute-done((bf16[64,24,128]{2,1,0:T(8,128)(2,1)}, bf16[64,24,128]{2,1,0:T(8,128)(2,1)S(1)}, u32[]{:S(2)}, u32[]{:S(2)}) %collective-permute-start.22) | collective-permute-done | bytes 393248 | tf_op jit(solution)/shard_map/ppermute | solution.py:533
  304.5 19.5 %all-to-all-start.5 = ((f32[64,1,128]{2,1,0:T(1,128)}), f32[64,1,128]{2,1,0:T(1,128)}, u32[]{:S(2)}, u32[]{:S(2)}) async-start(f32[64,1,128]{2,1,0:T(1,128)} %broadcast_in_dim.34), calls=%async_computation.5 | async-start | bytes 65536 | tf_op jit(solution)/shard_map/all_to_all | solution.py:529
  325.5 14.1 %shard_map.133.refs_4_ = f32[2,8192,128]{2,1,0:T(8,128)} custom-call(s32[2]{0:T(128)S(1)} %copy-done.16, f32[4]{0:T(128)S(1)} %get-tuple-element.99.weight_ref, s32[2,24,128]{2,1,0:T(8,128)S(1)} %copy-done.12, s32[2,128]{1,0:T(2,128)S(1)} %get-tuple-element.90.clash_ref, bf16[64,48,128]{2,1,0:T(8,128)(2,1)S(1)} %all-to-all-done.2.refs_0_, ...), custom_call_target="tpu_custom_call" | custom-call | tf_op jit(solution)/shard_map/pallas_call | solution.py:376
  339.6 13.9 %shard_map.134.refs_4_ = f32[2,8192,128]{2,1,0:T(8,128)} custom-call(s32[2]{0:T(128)S(1)} %copy-done.16, f32[4]{0:T(128)S(1)} %get-tuple-element.99.weight_ref, s32[2,24,128]{2,1,0:T(8,128)S(1)} %copy-done.13, s32[2,128]{1,0:T(2,128)S(1)} %get-tuple-element.91.clash_ref, ...), custom_call_target="tpu_custom_call", output_to_operand_aliasing={{}: (8, {})} | custom-call | tf_op jit(solution)/shard_map/pallas_call | solution.py:376
  354.9 1.3 slice.295
  357.9 15.8 %shard_map.135.refs_4_ = f32[2,8192,128]{2,1,0:T(8,128)} custom-call(s32[2]{0:T(128)S(1)} %copy-done.16, f32[4]{0:T(128)S(1)} %get-tuple-element.99.weight_ref, s32[2,24,128]{2,1,0:T(8,128)S(1)} %copy-done.9, s32[2,128]{1,0:T(2,128)S(1)} %get-tuple-element.92.clash_ref, ...), custom_call_target="tpu_custom_call", output_to_operand_aliasing={{}: (8, {})} | custom-call | tf_op jit(solution)/shard_map/pallas_call | solution.py:376
  373.8 15.9 %shard_map.136 = f32[2,8192,128]{2,1,0:T(8,128)} custom-call(s32[2]{0:T(128)S(1)} %copy-done.16, f32[4]{0:T(128)S(1)} %get-tuple-element.99.weight_ref, s32[2,24,128]{2,1,0:T(8,128)S(1)} %copy-done.8, s32[2,128]{1,0:T(2,128)S(1)} %get-tuple-element.93.clash_ref, bf16[64,24,128]{2,1,0:T(8,128)(2,1)S(1)} %get-tuple-element.69.refs_0_, ...), custom_call_target="tpu_custom_call", output_to_operand_aliasing={{}: (8, {})} | custom-call | tf_op jit(solution)/shard_map/pallas_call | solution.py:376
  (176 shorter events, 26.0 us)
Async XLA Ops:
  1.4 19.6 %collective-permute-start.3 = (bf16[8,1024]{1,0:T(8,128)(2,1)S(1)}, bf16[8,1024]{1,0:T(8,128)(2,1)S(1)}, u32[]{:S(2)}, u32[]{:S(2)}) collective-permute-start(bf16[8,1024]{1,0:T(8,128)(2,1)S(1)} %get-tuple-element.67), channel_id=1, source_target_pairs={{0,2},{1,3},{2,0},{3,1},{4,6},{5,7},{6,4},{7,5},{8,10},{9,11},{10,... | collective-permute-start | bytes 49160 | tf_op jit(solution)/shard_map/ppermute | solution.py:541
  8.4 21.0 %all-to-all-start = ((s32[64,1,96]{2,1,0:T(1,128)}), s32[64,1,96]{2,1,0:T(1,128)S(1)}, u32[]{:S(2)}, u32[]{:S(2)}) async-start(s32[64,1,96]{2,1,0:T(1,128)} %bitcast.3), calls=%async_computation | async-start | bytes 65536 | tf_op jit(solution)/shard_map/all_to_all | solution.py:529
  21.0 59.5 %copy-start.25 = (f32[64,128]{1,0:T(8,128)}, f32[64,128]{1,0:T(8,128)S(1)}, u32[]{:S(2)}) copy-start(f32[64,128]{1,0:T(8,128)S(1)} %maximum_maximum_fusion) | copy-start | bytes 98308
  21.0 20.9 %collective-permute-start.4 = (bf16[16,1024]{1,0:T(8,128)(2,1)S(1)}, bf16[16,1024]{1,0:T(8,128)(2,1)S(1)}, u32[]{:S(2)}, u32[]{:S(2)}) collective-permute-start(bf16[16,1024]{1,0:T(8,128)(2,1)S(1)} %pad_maximum_fusion.2), channel_id=1, source_target_pairs={{0,4},{1,5},{2,6},{3,7},{4,0},{5,1},{6,2},{7,3},{8,12},{9,13},{10,... | collective-permute-start | bytes 98312 | tf_op jit(solution)/shard_map/ppermute | solution.py:541
  29.5 7.6 %copy-start.22 = (s32[64,1,96]{2,1,0:T(1,128)}, s32[64,1,96]{2,1,0:T(1,128)S(1)}, u32[]{:S(2)}) copy-start(s32[64,1,96]{2,1,0:T(1,128)S(1)} %all-to-all-done) | copy-start | bytes 73732
  30.4 6.6 %copy-start.6 = (s32[48,128]{1,0:T(8,128)}, s32[48,128]{1,0:T(8,128)S(1)}, u32[]{:S(2)}) copy-start(s32[48,128]{1,0:T(8,128)S(1)} %get-tuple-element.44.idx_ref) | copy-start | bytes 73732
  30.4 2.2 copy-start
  37.1 42.7 %copy-start.30 = (s32[1,2,128]{2,1,0:T(2,128)S(1)}, s32[1,2,128]{2,1,0:T(2,128)}, u32[]{:S(2)}) copy-start(s32[1,2,128]{2,1,0:T(2,128)} %param.17) | copy-start | bytes 3076
  37.1 43.5 %copy-start.29 = (s32[1,2,2,1,128]{4,3,2,1,0:T(1,128)S(1)}, s32[1,2,2,1,128]{4,3,2,1,0:T(1,128)}, u32[]{:S(2)}) copy-start(s32[1,2,2,1,128]{4,3,2,1,0:T(1,128)} %param.15) | copy-start | bytes 6148
  37.1 49.7 %all-to-all-start.1 = ((bf16[64,48,128]{2,1,0:T(8,128)(2,1)}), bf16[64,48,128]{2,1,0:T(8,128)(2,1)S(1)}, u32[]{:S(2)}, u32[]{:S(2)}) async-start(bf16[64,48,128]{2,1,0:T(8,128)(2,1)} %bitcast.15), calls=%async_computation.1 | async-start | bytes 1572864 | tf_op jit(solution)/shard_map/all_to_all | solution.py:529
  41.9 24.2 %collective-permute-start.5 = (bf16[32,1024]{1,0:T(8,128)(2,1)S(1)}, bf16[32,1024]{1,0:T(8,128)(2,1)S(1)}, u32[]{:S(2)}, u32[]{:S(2)}) collective-permute-start(bf16[32,1024]{1,0:T(8,128)(2,1)S(1)} %pad_maximum_fusion.1), channel_id=1, source_target_pairs={{0,8},{1,9},{2,10},{3,11},{4,12},{5,13},{6,14},{7,15},{8,0},{9,1},... | collective-permute-start | bytes 196616 | tf_op jit(solution)/shard_map/ppermute | solution.py:541
  66.1 4.0 %collective-permute-start.6 = (bf16[64,1024]{1,0:T(8,128)(2,1)S(1)}, bf16[64,1024]{1,0:T(8,128)(2,1)S(1)}, u32[]{:S(2)}, u32[]{:S(2)}) collective-permute-start(bf16[64,1024]{1,0:T(8,128)(2,1)S(1)} %pad_maximum_fusion), channel_id=1, source_target_pairs={{0,16},{1,17},{2,18},{3,19},{4,20},{5,21},{6,22},{7,23},{8,24},{9,... | collective-permute-start | bytes 393224 | tf_op jit(solution)/shard_map/ppermute | solution.py:541
  67.5 8.3 %collective-permute-start.7 = (bf16[64,1024]{1,0:T(8,128)(2,1)S(1)}, bf16[64,1024]{1,0:T(8,128)(2,1)S(1)}, u32[]{:S(2)}, u32[]{:S(2)}) collective-permute-start(bf16[64,1024]{1,0:T(8,128)(2,1)S(1)} %pad_maximum_fusion), channel_id=1, source_target_pairs={{0,32},{1,33},{2,34},{3,35},{4,36},{5,37},{6,38},{7,39},{8,40},{9,... | collective-permute-start | bytes 393224 | tf_op jit(solution)/shard_map/ppermute | solution.py:541
  70.1 8.3 %collective-permute-start.8 = (bf16[64,1024]{1,0:T(8,128)(2,1)S(1)}, bf16[64,1024]{1,0:T(8,128)(2,1)S(1)}, u32[]{:S(2)}, u32[]{:S(2)}) collective-permute-start(bf16[64,1024]{1,0:T(8,128)(2,1)S(1)} %pad_maximum_fusion), channel_id=1, source_target_pairs={{0,48},{1,49},{2,50},{3,51},{4,52},{5,53},{6,54},{7,55},{8,56},{9,... | collective-permute-start | bytes 393224 | tf_op jit(solution)/shard_map/ppermute | solution.py:541
  78.4 8.4 %collective-permute-start.9 = (bf16[256,1024]{1,0:T(8,128)(2,1)S(1)}, bf16[256,1024]{1,0:T(8,128)(2,1)S(1)}, u32[]{:S(2)}, u32[]{:S(2)}) collective-permute-start(bf16[256,1024]{1,0:T(8,128)(2,1)S(1)} %constant_dynamic-update-slice_fusion.wa_ref), channel_id=1, source_target_pairs={{0,1},{1,0},{2,3},{3,2},{4,5},{5,4},{6,7},{7,6},{8,9},{9,8},{10,11... | collective-permute-start | bytes 1572872 | tf_op jit(solution)/shard_map/ppermute | solution.py:541
  94.2 2.0 collective-permute-start.10
  96.4 5.0 %collective-permute-start.11 = (bf16[64,1024]{1,0:T(8,128)(2,1)S(1)}, bf16[64,1024]{1,0:T(8,128)(2,1)S(1)}, u32[]{:S(2)}, u32[]{:S(2)}) collective-permute-start(bf16[64,1024]{1,0:T(8,128)(2,1)S(1)} %get-tuple-element.73), channel_id=1, source_target_pairs={{0,16},{1,17},{2,18},{3,19},{4,20},{5,21},{6,22},{7,23},{8,24},{9,... | collective-permute-start | bytes 393224 | tf_op jit(solution)/shard_map/ppermute | solution.py:541
  96.5 7.6 %collective-permute-start.12 = (bf16[64,1024]{1,0:T(8,128)(2,1)S(1)}, bf16[64,1024]{1,0:T(8,128)(2,1)S(1)}, u32[]{:S(2)}, u32[]{:S(2)}) collective-permute-start(bf16[64,1024]{1,0:T(8,128)(2,1)S(1)} %get-tuple-element.75), channel_id=1, source_target_pairs={{0,32},{1,33},{2,34},{3,35},{4,36},{5,37},{6,38},{7,39},{8,40},{9,... | collective-permute-start | bytes 393224 | tf_op jit(solution)/shard_map/ppermute | solution.py:541
  97.8 8.8 %collective-permute-start.13 = (bf16[64,1024]{1,0:T(8,128)(2,1)S(1)}, bf16[64,1024]{1,0:T(8,128)(2,1)S(1)}, u32[]{:S(2)}, u32[]{:S(2)}) collective-permute-start(bf16[64,1024]{1,0:T(8,128)(2,1)S(1)} %get-tuple-element.74), channel_id=1, source_target_pairs={{0,48},{1,49},{2,50},{3,51},{4,52},{5,53},{6,54},{7,55},{8,56},{9,... | collective-permute-start | bytes 393224 | tf_op jit(solution)/shard_map/ppermute | solution.py:541
  106.7 20.2 %copy-start.24 = (f32[6,1024]{1,0:T(8,128)S(1)}, f32[6,1024]{1,0:T(8,128)}, u32[]{:S(2)}) copy-start(f32[6,1024]{1,0:T(8,128)} %param.19) | copy-start | bytes 73732
  106.7 43.0 %copy-start.7 = (s32[48,128]{1,0:T(8,128)S(1)}, s32[48,128]{1,0:T(8,128)}, u32[]{:S(2)}) copy-start(s32[48,128]{1,0:T(8,128)} %copy-done.6) | copy-start | bytes 73732
  106.7 43.0 %copy-start.21 = (s32[1,128]{1,0:T(1,128)S(1)}, s32[1,128]{1,0:T(1,128)}, u32[]{:S(2)}) copy-start(s32[1,128]{1,0:T(1,128)} %copy-done.20) | copy-start | bytes 1540
  106.8 7.2 %collective-permute-start.14 = (bf16[32,1024]{1,0:T(8,128)(2,1)S(1)}, bf16[32,1024]{1,0:T(8,128)(2,1)S(1)}, u32[]{:S(2)}, u32[]{:S(2)}) collective-permute-start(bf16[32,1024]{1,0:T(8,128)(2,1)S(1)} %slice.352), channel_id=1, source_target_pairs={{0,8},{1,9},{2,10},{3,11},{4,12},{5,13},{6,14},{7,15},{8,0},{9,1},... | collective-permute-start | bytes 196616 | tf_op jit(solution)/shard_map/ppermute | solution.py:541
  114.0 12.8 %collective-permute-start.15 = (f32[8,1024]{1,0:T(8,128)S(1)}, f32[8,1024]{1,0:T(8,128)S(1)}, u32[]{:S(2)}, u32[]{:S(2)}) collective-permute-start(f32[8,1024]{1,0:T(8,128)S(1)} %get-tuple-element.79), channel_id=1, source_target_pairs={{0,2},{1,3},{2,0},{3,1},{4,6},{5,7},{6,4},{7,5},{8,10},{9,11},{10,... | collective-permute-start | bytes 98312 | tf_op jit(solution)/shard_map/ppermute | solution.py:541
  116.1 10.7 %collective-permute-start.16 = (f32[8,1024]{1,0:T(8,128)S(1)}, f32[8,1024]{1,0:T(8,128)S(1)}, u32[]{:S(2)}, u32[]{:S(2)}) collective-permute-start(f32[8,1024]{1,0:T(8,128)S(1)} %get-tuple-element.81), channel_id=1, source_target_pairs={{0,4},{1,5},{2,6},{3,7},{4,0},{5,1},{6,2},{7,3},{8,12},{9,13},{10,... | collective-permute-start | bytes 98312 | tf_op jit(solution)/shard_map/ppermute | solution.py:541
  116.1 10.7 %collective-permute-start.17 = (f32[8,1024]{1,0:T(8,128)S(1)}, f32[8,1024]{1,0:T(8,128)S(1)}, u32[]{:S(2)}, u32[]{:S(2)}) collective-permute-start(f32[8,1024]{1,0:T(8,128)S(1)} %get-tuple-element.80), channel_id=1, source_target_pairs={{0,6},{1,7},{2,4},{3,5},{4,2},{5,3},{6,0},{7,1},{8,14},{9,15},{10,... | collective-permute-start | bytes 98312 | tf_op jit(solution)/shard_map/ppermute | solution.py:541
  118.4 31.2 %all-to-all-start.2 = ((bf16[64,48,128]{2,1,0:T(8,128)(2,1)}), bf16[64,48,128]{2,1,0:T(8,128)(2,1)S(1)}, u32[]{:S(2)}, u32[]{:S(2)}) async-start(bf16[64,48,128]{2,1,0:T(8,128)(2,1)} %bitcast.17), calls=%async_computation.2 | async-start | bytes 1572864 | tf_op jit(solution)/shard_map/all_to_all | solution.py:529
  159.1 40.4 %copy-start.27 = (f32[1,1,128,13]{2,1,3,0:T(1,128)S(1)}, f32[1,1,128,13]{2,1,3,0:T(1,128)}, u32[]{:S(2)}) copy-start(f32[1,1,128,13]{2,1,3,0:T(1,128)} %get-tuple-element.87) | copy-start | bytes 19972
  159.1 40.5 %copy-start.28 = (f32[128,1]{0,1:T(1,128)S(1)}, f32[128,1]{0,1:T(1,128)}, u32[]{:S(2)}) copy-start(f32[128,1]{0,1:T(1,128)} %get-tuple-element.97) | copy-start | bytes 1540
  159.1 40.6 %copy-start.17 = (s32[2,512]{1,0:T(2,128)S(1)}, s32[2,512]{1,0:T(2,128)}, u32[]{:S(2)}) copy-start(s32[2,512]{1,0:T(2,128)} %get-tuple-element.89.slot_ref) | copy-start | bytes 12292
  159.1 40.6 %copy-start.19 = (s32[2,128]{1,0:T(2,128)S(1)}, s32[2,128]{1,0:T(2,128)}, u32[]{:S(2)}) copy-start(s32[2,128]{1,0:T(2,128)} %get-tuple-element.95.bag_ref) | copy-start | bytes 3076
  159.2 44.6 %copy-start.16 = (s32[2]{0:T(128)S(1)}, s32[2]{0:T(128)}, u32[]{:S(2)}) copy-start(s32[2]{0:T(128)} %copy-done.14) | copy-start | bytes 28
  199.4 4.3 %collective-permute-start.18 = (bf16[64,32,128]{2,1,0:T(8,128)(2,1)S(1)}, bf16[64,32,128]{2,1,0:T(8,128)(2,1)S(1)}, u32[]{:S(2)}, u32[]{:S(2)}) collective-permute-start(bf16[64,32,128]{2,1,0:T(8,128)(2,1)S(1)} %slice.279), channel_id=1, source_target_pairs={{0,1},{1,0},{2,3},{3,2},{4,5},{5,4},{6,7},{7,6},{8,9},{9,8},{10,11... | collective-permute-start | bytes 1572872 | tf_op jit(solution)/shard_map/ppermute | solution.py:541
  210.6 6.9 %collective-permute-start.28 = (bf16[256,1024]{1,0:T(8,128)(2,1)S(1)}, bf16[256,1024]{1,0:T(8,128)(2,1)}, u32[]{:S(2)}, u32[]{:S(2)}) collective-permute-start(bf16[256,1024]{1,0:T(8,128)(2,1)S(1)} %get-tuple-element.59), channel_id=1, source_target_pairs={{0,1},{1,0},{2,3},{3,2},{4,5},{5,4},{6,7},{7,6},{8,9},{9,8},{10,11... | collective-permute-start | bytes 1572872 | tf_op jit(solution)/shard_map/ppermute | solution.py:541
  211.2 48.2 %all-to-all-start.4 = ((bf16[64,48,128]{2,1,0:T(8,128)(2,1)}), bf16[64,48,128]{2,1,0:T(8,128)(2,1)}, u32[]{:S(2)}, u32[]{:S(2)}) async-start(bf16[64,48,128]{2,1,0:T(8,128)(2,1)} %bitcast.21), calls=%async_computation.4 | async-start | bytes 1572864 | tf_op jit(solution)/shard_map/all_to_all | solution.py:529
  217.5 5.6 %copy-start.31 = (s32[16]{0:T(128)S(1)}, s32[16]{0:T(128)}, u32[]{:S(2)}) copy-start(s32[16]{0:T(128)} %param.21) | copy-start | bytes 196
  218.8 24.1 %copy-start.23 = (s32[64,1,96]{2,1,0:T(1,128)S(1)}, s32[64,1,96]{2,1,0:T(1,128)}, u32[]{:S(2)}) copy-start(s32[64,1,96]{2,1,0:T(1,128)} %copy-done.22) | copy-start | bytes 73732
  218.9 6.8 %collective-permute-start.29 = (bf16[64,1024]{1,0:T(8,128)(2,1)S(1)}, bf16[64,1024]{1,0:T(8,128)(2,1)S(1)}, u32[]{:S(2)}, u32[]{:S(2)}) collective-permute-start(bf16[64,1024]{1,0:T(8,128)(2,1)S(1)} %get-tuple-element.70), channel_id=1, source_target_pairs={{0,16},{1,17},{2,18},{3,19},{4,20},{5,21},{6,22},{7,23},{8,24},{9,... | collective-permute-start | bytes 393224 | tf_op jit(solution)/shard_map/ppermute | solution.py:541
  220.5 13.4 %collective-permute-start.30 = (bf16[64,1024]{1,0:T(8,128)(2,1)S(1)}, bf16[64,1024]{1,0:T(8,128)(2,1)S(1)}, u32[]{:S(2)}, u32[]{:S(2)}) collective-permute-start(bf16[64,1024]{1,0:T(8,128)(2,1)S(1)} %get-tuple-element.72), channel_id=1, source_target_pairs={{0,32},{1,33},{2,34},{3,35},{4,36},{5,37},{6,38},{7,39},{8,40},{9,... | collective-permute-start | bytes 393224 | tf_op jit(solution)/shard_map/ppermute | solution.py:541
  223.1 13.8 %collective-permute-start.31 = (bf16[64,1024]{1,0:T(8,128)(2,1)S(1)}, bf16[64,1024]{1,0:T(8,128)(2,1)S(1)}, u32[]{:S(2)}, u32[]{:S(2)}) collective-permute-start(bf16[64,1024]{1,0:T(8,128)(2,1)S(1)} %get-tuple-element.71), channel_id=1, source_target_pairs={{0,48},{1,49},{2,50},{3,51},{4,52},{5,53},{6,54},{7,55},{8,56},{9,... | collective-permute-start | bytes 393224 | tf_op jit(solution)/shard_map/ppermute | solution.py:541
  236.9 10.9 %collective-permute-start.32 = (bf16[32,1024]{1,0:T(8,128)(2,1)S(1)}, bf16[32,1024]{1,0:T(8,128)(2,1)S(1)}, u32[]{:S(2)}, u32[]{:S(2)}) collective-permute-start(bf16[32,1024]{1,0:T(8,128)(2,1)S(1)} %slice.351), channel_id=1, source_target_pairs={{0,8},{1,9},{2,10},{3,11},{4,12},{5,13},{6,14},{7,15},{8,0},{9,1},... | collective-permute-start | bytes 196616 | tf_op jit(solution)/shard_map/ppermute | solution.py:541
  242.9 6.7 %collective-permute-start = (s32[64,96]{1,0:T(8,128)S(1)}, s32[64,96]{1,0:T(8,128)S(1)}, u32[]{:S(2)}, u32[]{:S(2)}) collective-permute-start(s32[64,96]{1,0:T(8,128)S(1)} %bitcast.56), channel_id=1, source_target_pairs={{0,64},{64,128},{128,192},{192,0},{1,65},{65,129},{129,193},{193,1... | collective-permute-start | bytes 73736 | tf_op jit(solution)/shard_map/ppermute | solution.py:533
  244.2 7.3 %collective-permute-start.1 = (s32[64,96]{1,0:T(8,128)S(1)}, s32[64,96]{1,0:T(8,128)S(1)}, u32[]{:S(2)}, u32[]{:S(2)}) collective-permute-start(s32[64,96]{1,0:T(8,128)S(1)} %bitcast.57), channel_id=1, source_target_pairs={{0,128},{64,192},{128,0},{192,64},{1,129},{65,193},{129,1},{193,65... | collective-permute-start | bytes 73736 | tf_op jit(solution)/shard_map/ppermute | solution.py:533
  246.7 4.8 %collective-permute-start.2 = (s32[64,96]{1,0:T(8,128)S(1)}, s32[64,96]{1,0:T(8,128)S(1)}, u32[]{:S(2)}, u32[]{:S(2)}) collective-permute-start(s32[64,96]{1,0:T(8,128)S(1)} %bitcast.58), channel_id=1, source_target_pairs={{0,192},{64,0},{128,64},{192,128},{1,193},{65,1},{129,65},{193,129... | collective-permute-start | bytes 73736 | tf_op jit(solution)/shard_map/ppermute | solution.py:533
  247.9 7.7 %collective-permute-start.33 = (f32[8,1024]{1,0:T(8,128)S(1)}, f32[8,1024]{1,0:T(8,128)S(1)}, u32[]{:S(2)}, u32[]{:S(2)}) collective-permute-start(f32[8,1024]{1,0:T(8,128)S(1)} %get-tuple-element.76), channel_id=1, source_target_pairs={{0,2},{1,3},{2,0},{3,1},{4,6},{5,7},{6,4},{7,5},{8,10},{9,11},{10,... | collective-permute-start | bytes 98312 | tf_op jit(solution)/shard_map/ppermute | solution.py:541
  248.9 7.4 %collective-permute-start.34 = (f32[8,1024]{1,0:T(8,128)S(1)}, f32[8,1024]{1,0:T(8,128)S(1)}, u32[]{:S(2)}, u32[]{:S(2)}) collective-permute-start(f32[8,1024]{1,0:T(8,128)S(1)} %get-tuple-element.78), channel_id=1, source_target_pairs={{0,4},{1,5},{2,6},{3,7},{4,0},{5,1},{6,2},{7,3},{8,12},{9,13},{10,... | collective-permute-start | bytes 98312 | tf_op jit(solution)/shard_map/ppermute | solution.py:541
  249.6 6.7 %collective-permute-start.35 = (f32[8,1024]{1,0:T(8,128)S(1)}, f32[8,1024]{1,0:T(8,128)S(1)}, u32[]{:S(2)}, u32[]{:S(2)}) collective-permute-start(f32[8,1024]{1,0:T(8,128)S(1)} %get-tuple-element.77), channel_id=1, source_target_pairs={{0,6},{1,7},{2,4},{3,5},{4,2},{5,3},{6,0},{7,1},{8,14},{9,15},{10,... | collective-permute-start | bytes 98312 | tf_op jit(solution)/shard_map/ppermute | solution.py:541
  253.6 41.1 %collective-permute-start.25 = (bf16[64,48,128]{2,1,0:T(8,128)(2,1)S(1)}, bf16[64,48,128]{2,1,0:T(8,128)(2,1)S(1)}, u32[]{:S(2)}, u32[]{:S(2)}) collective-permute-start(bf16[64,48,128]{2,1,0:T(8,128)(2,1)S(1)} %all-to-all-done.2.refs_0_), channel_id=1, source_target_pairs={{0,64},{64,128},{128,192},{192,0},{1,65},{65,129},{129,193},{193,1... | collective-permute-start | bytes 2359304 | tf_op jit(solution)/shard_map/ppermute | solution.py:533
  253.9 42.7 %collective-permute-start.26 = (bf16[64,48,128]{2,1,0:T(8,128)(2,1)S(1)}, bf16[64,48,128]{2,1,0:T(8,128)(2,1)S(1)}, u32[]{:S(2)}, u32[]{:S(2)}) collective-permute-start(bf16[64,48,128]{2,1,0:T(8,128)(2,1)S(1)} %all-to-all-done.2.refs_0_), channel_id=1, source_target_pairs={{0,128},{64,192},{128,0},{192,64},{1,129},{65,193},{129,1},{193,65... | collective-permute-start | bytes 2359304 | tf_op jit(solution)/shard_map/ppermute | solution.py:533
  255.6 41.7 %collective-permute-start.27 = (bf16[64,48,128]{2,1,0:T(8,128)(2,1)S(1)}, bf16[64,48,128]{2,1,0:T(8,128)(2,1)S(1)}, u32[]{:S(2)}, u32[]{:S(2)}) collective-permute-start(bf16[64,48,128]{2,1,0:T(8,128)(2,1)S(1)} %all-to-all-done.2.refs_0_), channel_id=1, source_target_pairs={{0,192},{64,0},{128,64},{192,128},{1,193},{65,1},{129,65},{193,129... | collective-permute-start | bytes 2359304 | tf_op jit(solution)/shard_map/ppermute | solution.py:533
  257.0 31.3 %collective-permute-start.36 = (f32[8,1024]{1,0:T(8,128)}, f32[8,1024]{1,0:T(8,128)}, u32[]{:S(2)}, u32[]{:S(2)}) collective-permute-start(f32[8,1024]{1,0:T(8,128)} %fusion.7), channel_id=1, source_target_pairs={{0,128},{64,192},{128,0},{192,64},{1,129},{65,193},{129,1},{193,65... | collective-permute-start | bytes 98312 | tf_op jit(solution)/shard_map/ppermute | solution.py:533
  259.3 31.8 %collective-permute-start.37 = (f32[8,1024]{1,0:T(8,128)}, f32[8,1024]{1,0:T(8,128)}, u32[]{:S(2)}, u32[]{:S(2)}) collective-permute-start(f32[8,1024]{1,0:T(8,128)} %fusion.7), channel_id=1, source_target_pairs={{0,64},{64,128},{128,192},{192,0},{1,65},{65,129},{129,193},{193,1... | collective-permute-start | bytes 98312 | tf_op jit(solution)/shard_map/ppermute | solution.py:533
  259.3 31.8 %copy-start.11 = (s32[4,2,24,128]{3,2,1,0:T(8,128)S(1)}, s32[4,2,24,128]{3,2,1,0:T(8,128)}, u32[]{:S(2)}) copy-start(s32[4,2,24,128]{3,2,1,0:T(8,128)} %copy-done.10) | copy-start | bytes 294916
  288.3 4.2 %collective-permute-start.38 = (f32[8,1024]{1,0:T(8,128)}, f32[8,1024]{1,0:T(8,128)S(1)}, u32[]{:S(2)}, u32[]{:S(2)}) collective-permute-start(f32[8,1024]{1,0:T(8,128)} %fusion.7), channel_id=1, source_target_pairs={{0,192},{64,0},{128,64},{192,128},{1,193},{65,1},{129,65},{193,129... | collective-permute-start | bytes 98312 | tf_op jit(solution)/shard_map/ppermute | solution.py:533
  291.1 11.9 %collective-permute-start.22 = (bf16[64,24,128]{2,1,0:T(8,128)(2,1)}, bf16[64,24,128]{2,1,0:T(8,128)(2,1)S(1)}, u32[]{:S(2)}, u32[]{:S(2)}) collective-permute-start(bf16[64,24,128]{2,1,0:T(8,128)(2,1)} %get-tuple-element.68.refs_0_), channel_id=1, source_target_pairs={{0,64},{64,128},{128,192},{192,0},{1,65},{65,129},{129,193},{193,1... | collective-permute-start | bytes 1179656 | tf_op jit(solution)/shard_map/ppermute | solution.py:533
  293.3 10.6 %copy-start.26 = (f32[8,1024]{1,0:T(8,128)}, f32[8,1024]{1,0:T(8,128)S(1)}, u32[]{:S(2)}) copy-start(f32[8,1024]{1,0:T(8,128)S(1)} %add_add_fusion) | copy-start | bytes 98308
  293.3 62.8 %collective-permute-start.23 = (bf16[64,24,128]{2,1,0:T(8,128)(2,1)}, bf16[64,24,128]{2,1,0:T(8,128)(2,1)}, u32[]{:S(2)}, u32[]{:S(2)}) collective-permute-start(bf16[64,24,128]{2,1,0:T(8,128)(2,1)} %get-tuple-element.68.refs_0_), channel_id=1, source_target_pairs={{0,128},{64,192},{128,0},{192,64},{1,129},{65,193},{129,1},{193,65... | collective-permute-start | bytes 1179656 | tf_op jit(solution)/shard_map/ppermute | solution.py:533
  294.7 61.4 %collective-permute-start.24 = (bf16[64,24,128]{2,1,0:T(8,128)(2,1)}, bf16[64,24,128]{2,1,0:T(8,128)(2,1)}, u32[]{:S(2)}, u32[]{:S(2)}) collective-permute-start(bf16[64,24,128]{2,1,0:T(8,128)(2,1)} %get-tuple-element.68.refs_0_), channel_id=1, source_target_pairs={{0,192},{64,0},{128,64},{192,128},{1,193},{65,1},{129,65},{193,129... | collective-permute-start | bytes 1179656 | tf_op jit(solution)/shard_map/ppermute | solution.py:533
  296.7 77.1 %collective-permute-start.19 = (bf16[64,24,128]{2,1,0:T(8,128)(2,1)S(1)}, bf16[64,24,128]{2,1,0:T(8,128)(2,1)}, u32[]{:S(2)}, u32[]{:S(2)}) collective-permute-start(bf16[64,24,128]{2,1,0:T(8,128)(2,1)S(1)} %get-tuple-element.69.refs_0_), channel_id=1, source_target_pairs={{0,64},{64,128},{128,192},{192,0},{1,65},{65,129},{129,193},{193,1... | collective-permute-start | bytes 1179656 | tf_op jit(solution)/shard_map/ppermute | solution.py:533
  297.2 76.5 %collective-permute-start.20 = (bf16[64,24,128]{2,1,0:T(8,128)(2,1)S(1)}, bf16[64,24,128]{2,1,0:T(8,128)(2,1)}, u32[]{:S(2)}, u32[]{:S(2)}) collective-permute-start(bf16[64,24,128]{2,1,0:T(8,128)(2,1)S(1)} %get-tuple-element.69.refs_0_), channel_id=1, source_target_pairs={{0,128},{64,192},{128,0},{192,64},{1,129},{65,193},{129,1},{193,65... | collective-permute-start | bytes 1179656 | tf_op jit(solution)/shard_map/ppermute | solution.py:533
  303.8 69.9 %collective-permute-start.21 = (bf16[64,24,128]{2,1,0:T(8,128)(2,1)S(1)}, bf16[64,24,128]{2,1,0:T(8,128)(2,1)}, u32[]{:S(2)}, u32[]{:S(2)}) collective-permute-start(bf16[64,24,128]{2,1,0:T(8,128)(2,1)S(1)} %get-tuple-element.69.refs_0_), channel_id=1, source_target_pairs={{0,192},{64,0},{128,64},{192,128},{1,193},{65,1},{129,65},{193,129... | collective-permute-start | bytes 1179656 | tf_op jit(solution)/shard_map/ppermute | solution.py:533
  304.5 49.1 %all-to-all-start.5 = ((f32[64,1,128]{2,1,0:T(1,128)}), f32[64,1,128]{2,1,0:T(1,128)}, u32[]{:S(2)}, u32[]{:S(2)}) async-start(f32[64,1,128]{2,1,0:T(1,128)} %broadcast_in_dim.34), calls=%async_computation.5 | async-start | bytes 65536 | tf_op jit(solution)/shard_map/all_to_all | solution.py:529
  325.5 14.1 %copy-start.13 = (s32[2,24,128]{2,1,0:T(8,128)S(1)}, s32[2,24,128]{2,1,0:T(8,128)}, u32[]{:S(2)}) copy-start(s32[2,24,128]{2,1,0:T(8,128)} %get-tuple-element.83.idx_ref) | copy-start | bytes 73732
  357.9 15.9 %copy-start.8 = (s32[2,24,128]{2,1,0:T(8,128)S(1)}, s32[2,24,128]{2,1,0:T(8,128)}, u32[]{:S(2)}) copy-start(s32[2,24,128]{2,1,0:T(8,128)} %get-tuple-element.85.idx_ref) | copy-start | bytes 73732
  (12 other events, 10.9 us)
